TPU v7x, 512 devices: a 8x2x16 block of a 8x16x16 slice. The times are simulated.
512 devices in a mesh: groups: 2 (over y), seq: 16 (over z), head: 8 (over x), inner: 2 (over core).
Axes of the slice: x: 8, y: 2, z: 16, core: 2. Of those that a mesh axis runs over, the one named last changes fastest.
The devices are a block of a 8x16x16 slice.
Arguments:
- queries: bfloat16 [16384, 8, 8, 128], P(('groups', 'seq'), 'head', 'inner'), parts along dimension 0, may hold values from -120 to 120
- grad_out: bfloat16 [16384, 8, 8, 128], P(('groups', 'seq'), 'head', 'inner'), parts along dimension 0, may hold values from -6 to 6
- keys: bfloat16 [16384, 8, 128], P(('groups', 'seq'), 'head'), parts along dimension 0, may hold values from -6 to 6
- values: bfloat16 [16384, 8, 128], P(('groups', 'seq'), 'head'), parts along dimension 0, may hold values from -6 to 6
- indices: int32 [8, 256, 16], P('head', 'groups'), parts along dimension 1, may hold values from 0 to 127, as said below
- valid: int32 [8, 256, 16], P('head', 'groups'), parts along dimension 1, may hold values from 0 to 1
Outputs:
- grad_queries: bfloat16 [16384, 8, 8, 128], P(('groups', 'seq'), 'head', 'inner'), parts along dimension 0
- grad_keys: bfloat16 [16384, 8, 128], P(('groups', 'seq'), 'head'), parts along dimension 0
- grad_values: bfloat16 [16384, 8, 128], P(('groups', 'seq'), 'head'), parts along dimension 0
There are 2 independent parts, one for each index of `groups`. A program takes and returns all parts, laid end to end along the dimension named above; each array names one. Nothing has to cross between parts.
Inputs may be any that keep to these rules, and one draw needn't show every extreme that they name: `indices`: call blocks r * 8 to r * 8 + 7 run r. For every KV head and query block b: slot 0 names b and is valid; the valid slots name distinct blocks at most b; over all query blocks of run r, the valid slots name blocks of runs later than r never, and for each earlier run exactly 4 distinct blocks of it. Slots that are not valid name arbitrary blocks.
All inputs are finite; a program needn't handle non-finite values.
Results may differ from a plain program's by a relative error of at most 0.007.
Values may be sent and summed in bfloat16 or wider, within the bound.
A program may use at most 64 MiB of HBM per device.

v0:
```python
import math

import jax
import jax.numpy as jnp
from jax import lax
from jax.sharding import PartitionSpec as P

BLK = 64
TOPK = 16
CAP = 4


def sent_together(arrays, axis, dim, along):
    both = jnp.concatenate(arrays, axis=along)
    result, at, outs = (lax.all_gather(both, axis, axis=dim, tiled=True), 0, [])
    for a in arrays:
        outs.append(lax.slice_in_dim(result, at, at + a.shape[along], axis=along))
        at += a.shape[along]
    return tuple(outs)


def cut_along(x, dim, size):
    shape = x.shape
    parts = x.reshape(*shape[:dim], size, shape[dim] // size, *shape[dim + 1 :])
    return jnp.moveaxis(parts, dim, 0)


def summed_on_arrival(x, axis, dim):
    size = lax.axis_size(axis)
    parts = lax.all_to_all(cut_along(x, dim, size), axis, 0, 0, tiled=True)
    return jnp.sum(parts.astype(jnp.float32), axis=0)


def in_one_piece(arrays, axis, dim, along):
    widths = [a.shape[along] for a in arrays]
    both = jnp.concatenate(arrays, axis=along)
    result = summed_on_arrival(both, axis, dim)
    return tuple(jnp.split(result, [sum(widths[:k]) for k in range(1, len(widths))], axis=along))


def in_one_piece_2(arrays, axis, split_dim, concat_dim, along):
    ends, at = ([], 0)
    for a in arrays[:-1]:
        at += a.shape[along]
        ends.append(at)
    both = jnp.concatenate(arrays, axis=along)
    return tuple(
        jnp.split(
            lax.all_to_all(both, axis, split_axis=split_dim, concat_axis=concat_dim, tiled=True),
            ends,
            axis=along,
        )
    )


def sent_to_all(x, axis):
    copies = jnp.broadcast_to(x, (lax.axis_size(axis), *x.shape))
    return lax.all_to_all(copies, axis, split_axis=0, concat_axis=0, tiled=True)


def taken_together(x, axis):
    return sent_to_all(x, axis).sum(axis=0)


def packed_total(arrays, axis):
    ravelled, at, outs = (jnp.concatenate([a.reshape(-1) for a in arrays]), 0, [])
    subtotal = taken_together(ravelled, axis)
    for a in arrays:
        outs.append(subtotal[at : at + a.size].reshape(a.shape))
        at += a.size
    return tuple(outs)


def per_device(queries, grad_out, keys, values, indices, valid):
    tokens = queries.shape[0]
    heads_here = queries.shape[2]
    width = queries.shape[3]
    seq_count = lax.axis_size("seq")
    seq_here = lax.axis_index("seq")
    blocks_here = tokens // BLK
    total_blocks = indices.shape[1]
    scaling = 1.0 / math.sqrt(width)
    remote_rows = seq_count * CAP
    dest_rows = remote_rows + blocks_here
    picks_all = indices[0]
    valid_all = valid[0] > 0
    owner_all = picks_all // blocks_here
    local_all = picks_all % blocks_here
    my_picks = lax.dynamic_slice_in_dim(picks_all, seq_here * blocks_here, blocks_here, 0)
    my_valid = lax.dynamic_slice_in_dim(valid_all, seq_here * blocks_here, blocks_here, 0)
    my_owner = my_picks // blocks_here
    my_local = my_picks % blocks_here
    remote = my_valid & (my_owner != seq_here)
    block_ids = jnp.arange(total_blocks, dtype=jnp.int32)
    hits_in = (my_picks[:, :, None] == block_ids[None, None, :]) & remote[:, :, None]
    present_in = jnp.any(hits_in, axis=(0, 1)).reshape(seq_count, blocks_here)
    rank_in = jnp.cumsum(present_in.astype(jnp.int32), axis=1) - 1
    slot_ref = jnp.sum(jnp.where(hits_in, rank_in.reshape(-1)[None, None, :], 0), axis=2)
    row_index = jnp.where(remote, my_owner * CAP + slot_ref, remote_rows + my_local)
    source_run = block_ids // blocks_here
    incoming = valid_all & (owner_all == seq_here) & (source_run != seq_here)[:, None]
    hits_out = (
        local_all[:, :, None] == jnp.arange(blocks_here, dtype=jnp.int32)[None, None, :]
    ) & incoming[:, :, None]
    present_out = jnp.any(hits_out.reshape(seq_count, blocks_here * TOPK, blocks_here), axis=1)
    rank_out = jnp.cumsum(present_out.astype(jnp.int32), axis=1) - 1
    choose_out = present_out[:, None, :] & (
        rank_out[:, None, :] == jnp.arange(CAP, dtype=jnp.int32)[None, :, None]
    )
    wanted = my_picks.reshape(-1)
    blank = jnp.zeros((blocks_here * TOPK, BLK, width), jnp.bfloat16)
    carry = (blank, blank)
    key_piece, value_piece = sent_together((keys, values), "seq", 0, 1)
    count = key_piece.shape[0] // BLK
    relative = wanted
    inside = (relative >= 0) & (relative < count)
    relative = jnp.clip(relative, 0, count - 1)
    key_rows = jnp.take(key_piece[:, 0].reshape(count, BLK, width), relative, axis=0)
    value_rows = jnp.take(value_piece[:, 0].reshape(count, BLK, width), relative, axis=0)
    sel_keys = jnp.where(inside[:, None, None], key_rows, carry[0])
    sel_values = jnp.where(inside[:, None, None], value_rows, carry[1])
    group = math.gcd(blocks_here, max(1, 512 // (BLK * heads_here)))
    steps_count = blocks_here // group
    span = TOPK * BLK
    position = jnp.arange(BLK, dtype=jnp.int32)
    causal = position[None, :] <= position[:, None]
    block_global = seq_here * blocks_here + jnp.arange(blocks_here, dtype=jnp.int32)
    before = my_picks < block_global[:, None]
    same = my_picks == block_global[:, None]
    allowed = my_valid[:, None, :, None] & (
        before[:, None, :, None] | same[:, None, :, None] & causal[None, :, None, :]
    )
    allowed = allowed.reshape(steps_count, group, BLK, span)
    query_steps = queries[:, 0].reshape(steps_count, group, BLK, heads_here, width)
    grad_steps = grad_out[:, 0].reshape(steps_count, group, BLK, heads_here, width)
    key_steps = sel_keys.reshape(steps_count, group, span, width)
    value_steps = sel_values.reshape(steps_count, group, span, width)
    row_steps = row_index.reshape(steps_count, group * TOPK)

    def attend(carry, inputs):
        key_acc, value_acc = carry
        q_group, do_group, k_group, v_group, mask_group, rows_group = inputs
        mask_heads = mask_group[:, None, :, :]
        scores = (
            jnp.einsum("qigw,qsw->qgis", q_group, k_group, preferred_element_type=jnp.float32)
            * scaling
        )
        highest = jnp.max(jnp.where(mask_heads, scores, -jnp.inf), axis=-1, keepdims=True)
        weights = jnp.where(mask_heads, jnp.exp(scores - highest), 0.0)
        probs = weights / jnp.sum(weights, axis=-1, keepdims=True)
        probs_b = probs.astype(jnp.bfloat16)
        dprobs = jnp.einsum("qigw,qsw->qgis", do_group, v_group, preferred_element_type=jnp.float32)
        delta = jnp.sum(probs * dprobs, axis=-1, keepdims=True)
        dscores = (probs * (dprobs - delta)).astype(jnp.bfloat16)
        query_grad = (
            jnp.einsum("qgis,qsw->qigw", dscores, k_group, preferred_element_type=jnp.float32)
            * scaling
        ).astype(jnp.bfloat16)
        key_terms = (
            jnp.einsum("qgis,qigw->qsw", dscores, q_group, preferred_element_type=jnp.float32)
            * scaling
        )
        value_terms = jnp.einsum(
            "qgis,qigw->qsw", probs_b, do_group, preferred_element_type=jnp.float32
        )
        key_acc = key_acc.at[rows_group].add(key_terms.reshape(group * TOPK, BLK * width))
        value_acc = value_acc.at[rows_group].add(value_terms.reshape(group * TOPK, BLK * width))
        return ((key_acc, value_acc), query_grad)

    zeros_dest = jnp.zeros((dest_rows, BLK * width), jnp.float32)
    (key_acc, value_acc), query_grads = lax.scan(
        attend,
        (zeros_dest, zeros_dest),
        (query_steps, grad_steps, key_steps, value_steps, allowed, row_steps),
    )
    grad_queries = query_grads.reshape(tokens, 1, heads_here, width)
    send_key_tiles = key_acc[:remote_rows].reshape(seq_count, CAP, BLK * width)
    send_value_tiles = value_acc[:remote_rows].reshape(seq_count, CAP, BLK * width)
    own_keys = key_acc[remote_rows:]
    own_values = value_acc[remote_rows:]
    choose_float = choose_out.astype(jnp.float32)
    share = CAP // lax.axis_size("inner")
    summed_keys, summed_values = in_one_piece(
        (send_key_tiles.astype(jnp.bfloat16), send_value_tiles.astype(jnp.bfloat16)), "inner", 1, 0
    )
    back_keys, back_values = tuple(
        (
            part.astype(jnp.float32)
            for part in in_one_piece_2(
                (summed_keys.astype(jnp.bfloat16), summed_values.astype(jnp.bfloat16)),
                "seq",
                0,
                0,
                1,
            )
        )
    )
    mapping = lax.dynamic_slice_in_dim(choose_float, lax.axis_index("inner") * share, share, 1)
    local_keys = own_keys + jnp.einsum(
        "dcb,dcx->bx", mapping, back_keys, precision=lax.Precision.HIGHEST
    )
    local_values = own_values + jnp.einsum(
        "dcb,dcx->bx", mapping, back_values, precision=lax.Precision.HIGHEST
    )
    total_keys, total_values = packed_total((local_keys, local_values), "inner")
    grad_keys = total_keys.astype(jnp.bfloat16).reshape(tokens, 1, width)
    grad_values = total_values.astype(jnp.bfloat16).reshape(tokens, 1, width)
    return (grad_queries, grad_keys, grad_values)


def solution(mesh):
    return jax.shard_map(
        per_device,
        mesh=mesh,
        in_specs=(
            P(("groups", "seq"), "head", "inner", None),
            P(("groups", "seq"), "head", "inner", None),
            P(("groups", "seq"), "head", None),
            P(("groups", "seq"), "head", None),
            P("head", "groups", None),
            P("head", "groups", None),
        ),
        out_specs=(
            P(("groups", "seq"), "head", "inner", None),
            P(("groups", "seq"), "head", None),
            P(("groups", "seq"), "head", None),
        ),
        check_vma=False,
    )
```

profile of v0, /device:TPU:65, one launch (start us, length us, event | category | flops | bytes accessed | tf_op | source)
XLA Modules:
  0.0 339.7 jit_solution(4275878442553822181)
XLA Ops:
  14.6 101.6 %all-gather.2.cloned.1.call-done = bf16[8192,2,128]{2,0,1:T(8,128)(2,1)} async-done(((bf16[512,2,128]{2,0,1:T(8,128)(2,1)}), bf16[8192,2,128]{2,0,1:T(8,128)(2,1)}) %all-gather.2.cloned.1.call-update) | async-done | bytes 4194320 | tf_op jit(solution)/shard_map/all_gather | solution.py:15
  116.2 4.5 %fusion.59 = (bf16[8192,1,128]{2,0,1:T(8,128)(2,1)}, bf16[8192,1,128]{2,0,1:T(8,128)(2,1)}) fusion(bf16[8192,2,128]{2,0,1:T(8,128)(2,1)} %all-gather.2.cloned.1.call-done), kind=kLoop, calls=%fused_computation.126 | loop fusion | bytes 8388608 | tf_op jit(solution)/shard_map/slice | solution.py:17
  120.7 2.5 gather_fusion.1
  123.2 3.7 %gather_fusion = bf16[128,64,128]{2,1,0:T(8,128)(2,1)} fusion(bf16[128,64,128]{2,1,0:T(8,128)(2,1)} %bitcast.147, s32[1024]{0:T(1024)S(1)} %pad_clamp_fusion), kind=kCustom, calls=%fused_computation.clone | custom fusion | bytes 4194816 | tf_op jit(solution)/shard_map/jit(_take)/gather | solution.py:118
  127.0 3.7 %select_select_fusion = (bf16[128,64,128]{2,1,0:T(8,128)(2,1)}, bf16[128,64,128]{2,1,0:T(8,128)(2,1)}) fusion(bf16[128,64,128]{2,1,0:T(8,128)(2,1)S(1)} %gather_fusion.1, pred[128]{0:T(512)(128)(4,1)S(1)} %compare_and_fusion.2, pred[128]{0:T(512)(128)(4,1)S(1)} %and.167, bf16[128,64,128]{2,1,0:T(8,128)(2,1)} %gather_fusion), kind=kLoop, calls=%fused_computation.57 | loop fusion | flops 4194304 | bytes 8388864 | tf_op jit(solution)/shard_map/jit(_where)/select_n | solution.py:121
  132.4 97.8 %while.14 = (s32[]{:T(128)}, f32[72,8192]{1,0:T(8,128)}, f32[72,8192]{1,0:T(8,128)S(1)}, bf16[4,2,64,4,128]{4,3,2,1,0:T(4,128)(2,1)}, s32[4,32]{1,0:T(4,128)S(1)...) while((s32[]{:T(128)}, f32[72,8192]{1,0:T(8,128)}, ...), condition=%wide.region_9.11_spmd, body=%wide.region_3.10_spmd.sunk | while | flops 679871104 | bytes 53228260 | solution.py:171
  141.3 2.7 scatter_fusion.1
  144.0 2.5 fusion.84
  152.1 4.8 %scatter_fusion = f32[72,8192]{1,0:T(8,128)} fusion(f32[72,8192]{1,0:T(8,128)} %get-tuple-element.237, s32[32]{0:T(128)S(1)} %fusion.81, f32[32,8192]{1,0:T(8,128)S(1)} %reshape.374), kind=kCustom, calls=%fused_computation.2.clone.1 | custom fusion | flops 262144 | bytes 3145856 | tf_op jit(solution)/shard_map/while/body/eval_jaxpr/scatter-add | solution.py:166
  165.8 2.7 scatter_fusion.1
  168.5 2.5 fusion.84
  176.5 4.8 %scatter_fusion = f32[72,8192]{1,0:T(8,128)} fusion(f32[72,8192]{1,0:T(8,128)} %get-tuple-element.237, s32[32]{0:T(128)S(1)} %fusion.81, f32[32,8192]{1,0:T(8,128)S(1)} %reshape.374), kind=kCustom, calls=%fused_computation.2.clone.1 | custom fusion | flops 262144 | bytes 3145856 | tf_op jit(solution)/shard_map/while/body/eval_jaxpr/scatter-add | solution.py:166
  190.3 2.7 scatter_fusion.1
  192.9 2.5 fusion.84
  201.0 4.8 %scatter_fusion = f32[72,8192]{1,0:T(8,128)} fusion(f32[72,8192]{1,0:T(8,128)} %get-tuple-element.237, s32[32]{0:T(128)S(1)} %fusion.81, f32[32,8192]{1,0:T(8,128)S(1)} %reshape.374), kind=kCustom, calls=%fused_computation.2.clone.1 | custom fusion | flops 262144 | bytes 3145856 | tf_op jit(solution)/shard_map/while/body/eval_jaxpr/scatter-add | solution.py:166
  214.7 2.7 scatter_fusion.1
  217.4 2.5 fusion.84
  225.5 4.8 %scatter_fusion = f32[72,8192]{1,0:T(8,128)} fusion(f32[72,8192]{1,0:T(8,128)} %get-tuple-element.237, s32[32]{0:T(128)S(1)} %fusion.81, f32[32,8192]{1,0:T(8,128)S(1)} %reshape.374), kind=kCustom, calls=%fused_computation.2.clone.1 | custom fusion | flops 262144 | bytes 3145856 | tf_op jit(solution)/shard_map/while/body/eval_jaxpr/scatter-add | solution.py:166
  235.1 4.2 %maximum_bitcast_fusion = bf16[2,32,2,8192]{3,2,0,1:T(2,128)(2,1)S(1)} fusion(bf16[16,2,2,8192]{3,2,1,0:T(2,128)(2,1)} %convert_element_type.51, bf16[16,2,2,8192]{3,2,1,0:T(2,128)(2,1)} %convert_element_type.50), kind=kLoop, calls=%fused_computation.56 | loop fusion | flops 1048576 | bytes 4194304 | tf_op jit(solution)/shard_map/transpose | solution.py:25
  241.1 15.2 %all_to_all.16 = bf16[2,32,2,8192]{3,2,1,0:T(2,128)(2,1)} all-to-all(bf16[2,32,2,8192]{3,2,1,0:T(2,128)(2,1)S(1)} %copy.75), channel_id=1, replica_groups=mesh['groups'=2,'seq'=16,'head'=8,'inner'=2] {'inner'}, dimensions={0} | all-to-all | bytes 4194304 | tf_op jit(solution)/shard_map/all_to_all | solution.py:30
  256.3 5.3 %reduce.1 = bf16[32,2,8192]{2,1,0:T(2,128)(2,1)S(1)} reduce(bf16[2,32,2,8192]{3,2,1,0:T(2,128)(2,1)} %all_to_all.16, bf16[]{:T(256)} %constant.123.clone.1), dimensions={0}, to_apply=%region_12.14.clone | reduce | flops 524288 | bytes 3145730 | tf_op jit(solution)/shard_map/reduce_sum | solution.py:31
  264.5 7.2 %all-to-all-start.1 = ((bf16[16,4,8192]{2,1,0:T(4,128)(2,1)}), bf16[16,4,8192]{2,1,0:T(4,128)(2,1)S(1)}, u32[]{:S(2)}, u32[]{:S(2)}) async-start(bf16[16,4,8192]{2,1,0:T(4,128)(2,1)} %pad_maximum_fusion), calls=%async_computation.1 | async-start | bytes 2097152 | tf_op jit(solution)/shard_map/all_to_all | solution.py:49
  272.9 44.2 %all-to-all-done.1 = bf16[16,4,8192]{2,1,0:T(4,128)(2,1)S(1)} async-done(((bf16[16,4,8192]{2,1,0:T(4,128)(2,1)}), bf16[16,4,8192]{2,1,0:T(4,128)(2,1)S(1)}, u32[]{:S(2)}, u32[]{:S(2)}) %all-to-all-start.1) | async-done | bytes 1048608 | tf_op jit(solution)/shard_map/all_to_all | solution.py:49
  320.6 9.6 %all_to_all.17 = f32[2,1,131072]{2,1,0:T(1,128)S(1)} all-to-all(f32[2,1,131072]{2,1,0:T(1,128)S(1)} %broadcast_in_dim.100), channel_id=1, replica_groups=mesh['groups'=2,'seq'=16,'head'=8,'inner'=2] {'inner'}, dimensions={0} | all-to-all | bytes 2097152 | tf_op jit(solution)/shard_map/all_to_all | solution.py:58
  (147 shorter events, 83.5 us)
Async XLA Ops:
  7.2 109.0 %all-gather.2.cloned.1.call-start = ((), (), s32[]{:S(2)}) async-start(), calls=%async_computation.3 | async-start | bytes 4456448 | tf_op jit(solution)/shard_map/all_gather | solution.py:15
  9.8 3.2 copy-start.3
  11.1 0.6 copy-start.5
  134.4 2.4 copy-start.2
  136.9 1.3 copy-start
  144.0 2.5 copy-start.1
  158.9 2.4 copy-start.2
  161.3 1.3 copy-start
  168.5 2.5 copy-start.1
  183.4 2.4 copy-start.2
  185.8 1.3 copy-start
  192.9 2.5 copy-start.1
  207.8 2.4 copy-start.2
  210.2 1.3 copy-start
  217.4 2.5 copy-start.1
  262.4 9.3 %copy-start.4 = (s32[1,128,16]{2,1,0:T(8,128)S(1)}, s32[1,128,16]{2,1,0:T(8,128)}, u32[]{:S(2)}) copy-start(s32[1,128,16]{2,1,0:T(8,128)} %copy-done.3) | copy-start | bytes 24580
  262.4 9.4 %copy-start.6 = (pred[1,128,16]{2,1,0:T(8,128)(4,1)S(1)}, pred[1,128,16]{2,1,0:T(8,128)(4,1)}, u32[]{:S(2)}) copy-start(pred[1,128,16]{2,1,0:T(8,128)(4,1)} %copy-done.5) | copy-start | bytes 6148
  264.5 52.5 %all-to-all-start.1 = ((bf16[16,4,8192]{2,1,0:T(4,128)(2,1)}), bf16[16,4,8192]{2,1,0:T(4,128)(2,1)S(1)}, u32[]{:S(2)}, u32[]{:S(2)}) async-start(bf16[16,4,8192]{2,1,0:T(4,128)(2,1)} %pad_maximum_fusion), calls=%async_computation.1 | async-start | bytes 2097152 | tf_op jit(solution)/shard_map/all_to_all | solution.py:49
Sparse Core Ops, SparseCore 0:
  10.1 106.0 all-gather.1
where the time goes:
time: 341 us; the launch traced here: 340 us
  waiting for transfers between devices  146 us (43%)
  other arithmetic  56.3 us (17%)
  local copies, waits for them, and re-layouts  54 us (16%)
  matrix products  36.8 us (11%)
  blocking collectives  24.7 us (7%)
  between operations  14.4 us (4%)
  starting transfers between devices  7.28 us (2%)
    all_gather x1, waiting for transfers between devices, sent_together(): result, at, outs = (lax.all_gather(both, axis, axis=dim, tiled=True), 0, [])  102 us
    all_to_all x1, waiting for transfers between devices, in_one_piece_2(): lax.all_to_all(both, axis, split_axis=split_dim, concat_axis=concat_dim,...  44.2 us
    scatter-add x4, other arithmetic, attend(): key_acc.at[rows_group].add(key_terms.reshape(group * TOPK, BLK * width))  19.2 us
    all_to_all x1, blocking collectives, summed_on_arrival(): parts = lax.all_to_all(cut_along(x, dim, size), axis, 0, 0, tiled=True)  15.2 us
    scatter-add x4, other arithmetic, attend(): value_acc.at[rows_group].add(value_terms.reshape(group * TOPK, BLK * width))  10.6 us
    dot_general x4, matrix products, attend(): jnp.einsum('qigw,qsw->qgis', do_group, v_group, preferred_element_type=jn...  9.92 us
    all_to_all x1, blocking collectives, sent_to_all(): return lax.all_to_all(copies, axis, split_axis=0, concat_axis=0, tiled=True)  9.59 us
    all_to_all x1, starting transfers between devices, in_one_piece_2(): lax.all_to_all(both, axis, split_axis=split_dim, concat_axis=concat_dim,...  7.22 us
  transfers between devices with their start and end apart: 2, of which 2 were waited for; matrix products, arithmetic and copies ran while one was open for 2% of the time, Pallas kernels for 0%

commit v1 on v0

v1 whole, which is shorter than its diff:
```python
import functools
import math

import jax
import jax.numpy as jnp
from jax import lax
from jax.experimental import pallas as pl
from jax.experimental.pallas import tpu as pltpu
from jax.sharding import PartitionSpec as P

BLK = 64
TOPK = 16
SUB = 4
MESH = pl.DeviceIdType.MESH
LOG2E = 1.4426950408889634


def greet(axes_ids):
    barrier = pltpu.get_barrier_semaphore()
    for where in axes_ids:
        pl.semaphore_signal(barrier, inc=1, device_id=where, device_id_type=MESH)
    pl.semaphore_wait(barrier, len(axes_ids))


def places(n):
    me = lax.axis_index("seq")
    core = lax.axis_index("inner")
    up = {"seq": lax.rem(me + 1, n)}
    down = {"seq": lax.rem(me + n - 1, n)}
    partner = {"inner": 1 - core}
    return me, core, up, down, partner


def send(src, dst, s_sem, r_sem, where):
    return pltpu.make_async_remote_copy(
        src_ref=src, dst_ref=dst, send_sem=s_sem, recv_sem=r_sem, device_id=where, device_id_type=MESH
    )


def gather_kernel(n, k_ref, v_ref, kv_ref, local_sem, us, ur, ds, dr, ps, pr):
    me, core, up, down, partner = places(n)
    rows = k_ref.shape[0]
    part = rows // SUB
    n_up = n // 2
    n_down = n - 1 - n_up
    own_k = pltpu.make_async_copy(k_ref, kv_ref.at[0, me], local_sem.at[0])
    own_v = pltpu.make_async_copy(v_ref, kv_ref.at[1, me], local_sem.at[1])
    own_k.start()
    own_v.start()
    greet((up, down, partner))
    own_k.wait()
    own_v.wait()

    def piece(run, u):
        return kv_ref.at[core, run, pl.ds(u * part, part)]

    started = []

    def go_up(t, u):
        run = lax.rem(me - t + n, n)
        c = send(piece(run, u), piece(run, u), us.at[t * SUB + u], ur.at[t * SUB + u], up)
        c.start()
        started.append(c)
        return c

    def go_down(t, u):
        run = lax.rem(me + t, n)
        c = send(piece(run, u), piece(run, u), ds.at[t * SUB + u], dr.at[t * SUB + u], down)
        c.start()
        started.append(c)
        return c

    ups = [go_up(0, u) for u in range(SUB)]
    downs = [go_down(0, u) for u in range(SUB)]
    across = []

    def share(run, j):
        c = send(kv_ref.at[core, run], kv_ref.at[core, run], ps.at[j], pr.at[j], partner)
        c.start()
        across.append(c)

    for t in range(n_up):
        next_ups, next_downs = [], []
        for u in range(SUB):
            ups[u].wait_recv()
            if t + 1 < n_up:
                next_ups.append(go_up(t + 1, u))
            if t < n_down:
                downs[u].wait_recv()
                if t + 1 < n_down:
                    next_downs.append(go_down(t + 1, u))
        share(lax.rem(me - 1 - t + n, n), 2 * t)
        if t < n_down:
            share(lax.rem(me + 1 + t, n), 2 * t + 1)
        ups, downs = next_ups, next_downs
    for c in across:
        c.wait_recv()
    for c in started + across:
        c.wait_send()


def attend_kernel(scaling, picks, usable, q_ref, do_ref, kv_ref, dq_ref, mine_ref, theirs_ref, other):
    i = pl.program_id(0)
    core = lax.axis_index("inner")
    first = core == 0
    rows = q_ref.shape[0]
    per_pos = rows // BLK

    @pl.when(i == 0)
    def _():
        mine_ref[...] = jnp.zeros_like(mine_ref)
        other[...] = jnp.zeros_like(other)

    q = q_ref[...]
    do = do_ref[...]
    names = [picks[i, t] for t in range(TOPK)]
    ks = jnp.concatenate([kv_ref[0, b] for b in names], axis=0)
    vs = jnp.concatenate([kv_ref[1, b] for b in names], axis=0)
    nt = (((1,), (1,)), ((), ()))
    st = lax.dot_general(ks, q, nt, preferred_element_type=jnp.float32)
    key_at = lax.broadcasted_iota(jnp.int32, (BLK, rows), 0)
    query_at = lax.broadcasted_iota(jnp.int32, (BLK, rows), 1) // per_pos
    low = jnp.float32(-1e30)
    parts = [jnp.where(key_at <= query_at, st[:BLK], low)]
    for t in range(1, TOPK):
        bias = jnp.where(usable[i, t] > 0, jnp.float32(0.0), low)
        parts.append(st[t * BLK : (t + 1) * BLK] + bias)
    st = jnp.concatenate(parts, axis=0)
    top = jnp.max(st, axis=0, keepdims=True)
    w = jnp.exp2((st - top) * jnp.float32(scaling * LOG2E))
    inv = 1.0 / jnp.sum(w, axis=0, keepdims=True)
    p = w * inv
    dp = lax.dot_general(vs, do, nt, preferred_element_type=jnp.float32)
    delta = jnp.sum(p * dp, axis=0, keepdims=True)
    dsc = (p * (dp - delta)).astype(jnp.bfloat16)
    pb = p.astype(jnp.bfloat16)
    dqt = lax.dot_general(ks, dsc, (((0,), (0,)), ((), ())), preferred_element_type=jnp.float32)
    dq_ref[...] = (dqt.T * scaling).astype(jnp.bfloat16)
    dk = jnp.dot(dsc, q, preferred_element_type=jnp.float32) * scaling
    dv = jnp.dot(pb, do, preferred_element_type=jnp.float32)
    for t in range(TOPK):
        a = dk[t * BLK : (t + 1) * BLK]
        b = dv[t * BLK : (t + 1) * BLK]
        mine_ref[names[t]] += jnp.where(first, a, b)
        other[names[t]] += jnp.where(first, b, a)

    @pl.when(i == pl.num_programs(0) - 1)
    def _():
        theirs_ref[...] = other[...].astype(jnp.bfloat16)


def reduce_kernel(
    n, mine, theirs, out_k, out_v, peer, got_down, got_up, put_down, put_up, final,
    ds, dr, us, ur, ps, pr, fs, fr,
):
    me, core, up, down, partner = places(n)
    rows = mine.shape[1]
    part = rows // SUB
    n_down = n // 2
    n_up = n - 1 - n_down
    greet((up, down, partner))
    order = []
    for t in range(n_down):
        order.append(("d", t))
        if t < n_up:
            order.append(("u", t))
    order.append(("own", 0))
    hand = {}

    def run_of(kind, t):
        if kind == "d":
            return lax.rem(me - n_down + t + n, n)
        if kind == "u":
            return lax.rem(me + n_up - t, n)
        return me

    for j, key in enumerate(order):
        run = run_of(*key)
        c = send(theirs.at[run], peer.at[run], ps.at[j], pr.at[j], partner)
        c.start()
        hand[key] = c
    started = []

    def base(run, u):
        s = pl.ds(u * part, part)
        return mine[run, s, :] + peer[run, s, :].astype(jnp.float32)

    def step(t, u, kind, put, got, s_sem, r_sem, where):
        run = run_of(kind, t)
        val = base(run, u)
        s = pl.ds(u * part, part)
        if t > 0:
            val = val + got[t - 1, s, :].astype(jnp.float32)
        put[t, s, :] = val.astype(jnp.bfloat16)
        c = send(put.at[t, s], got.at[t, s], s_sem.at[t * SUB + u], r_sem.at[t * SUB + u], where)
        c.start()
        started.append(c)
        return c

    downs = ups = None
    for t in range(n_down):
        next_downs, next_ups = [], []
        hand[("d", t)].wait_recv()
        if t < n_up:
            hand[("u", t)].wait_recv()
        for u in range(SUB):
            if t > 0:
                downs[u].wait_recv()
            next_downs.append(step(t, u, "d", put_down, got_down, ds, dr, down))
            if t < n_up:
                if t > 0:
                    ups[u].wait_recv()
                next_ups.append(step(t, u, "u", put_up, got_up, us, ur, up))
        if t == n_up:
            last_ups = ups
        downs, ups = next_downs, next_ups
    hand[("own", 0)].wait_recv()
    finals = []
    for u in range(SUB):
        s = pl.ds(u * part, part)
        last_ups[u].wait_recv()
        downs[u].wait_recv()
        val = base(me, u) + got_down[n_down - 1, s, :].astype(jnp.float32)
        val = (val + got_up[n_up - 1, s, :].astype(jnp.float32)).astype(jnp.bfloat16)
        final[core, s, :] = val
        c = send(final.at[core, s], final.at[core, s], fs.at[u], fr.at[u], partner)
        c.start()
        finals.append(c)
    for c in finals:
        c.wait_recv()
    for c in list(hand.values()) + started + finals:
        c.wait_send()
    out_k[...] = final[0]
    out_v[...] = final[1]


def vmem():
    return pl.BlockSpec(memory_space=pltpu.VMEM)


def anywhere():
    return pl.BlockSpec(memory_space=pl.ANY)


def per_device(queries, grad_out, keys, values, indices, valid):
    tokens, _, heads_here, width = queries.shape
    n = lax.axis_size("seq")
    seq_here = lax.axis_index("seq")
    blocks = tokens // BLK
    total_blocks = n * blocks
    scaling = 1.0 / math.sqrt(width)
    rows = BLK * heads_here
    half = n // 2
    rest = n - 1 - half
    dma = pltpu.SemaphoreType.DMA
    bf16, f32 = jnp.bfloat16, jnp.float32
    picks = lax.dynamic_slice_in_dim(indices[0], seq_here * blocks, blocks, 0)
    usable = lax.dynamic_slice_in_dim(valid[0], seq_here * blocks, blocks, 0)

    kv = pl.pallas_call(
        functools.partial(gather_kernel, n),
        out_shape=jax.ShapeDtypeStruct((2, n, tokens, width), bf16),
        in_specs=[anywhere()] * 2,
        out_specs=vmem(),
        scratch_shapes=[
            dma((2,)),
            dma((half * SUB,)), dma((half * SUB,)),
            dma((rest * SUB,)), dma((rest * SUB,)),
            dma((2 * half,)), dma((2 * half,)),
        ],
        compiler_params=pltpu.CompilerParams(collective_id=1, has_side_effects=True),
    )(keys[:, 0], values[:, 0])

    q2 = queries.reshape(tokens * heads_here, width)
    do2 = grad_out.reshape(tokens * heads_here, width)
    whole = lambda i, *_: (0, 0, 0)
    dq, mine, theirs = pl.pallas_call(
        functools.partial(attend_kernel, scaling),
        out_shape=(
            jax.ShapeDtypeStruct((tokens * heads_here, width), bf16),
            jax.ShapeDtypeStruct((total_blocks, BLK, width), f32),
            jax.ShapeDtypeStruct((total_blocks, BLK, width), bf16),
        ),
        grid_spec=pltpu.PrefetchScalarGridSpec(
            num_scalar_prefetch=2,
            grid=(blocks,),
            in_specs=[
                pl.BlockSpec((rows, width), lambda i, *_: (i, 0)),
                pl.BlockSpec((rows, width), lambda i, *_: (i, 0)),
                pl.BlockSpec((2, total_blocks, BLK, width), lambda i, *_: (0, 0, 0, 0)),
            ],
            out_specs=[
                pl.BlockSpec((rows, width), lambda i, *_: (i, 0)),
                pl.BlockSpec((total_blocks, BLK, width), whole),
                pl.BlockSpec((total_blocks, BLK, width), whole),
            ],
            scratch_shapes=[pltpu.VMEM((total_blocks, BLK, width), f32)],
        ),
        compiler_params=pltpu.CompilerParams(
            dimension_semantics=("arbitrary",), vmem_limit_bytes=60 * 2**20
        ),
    )(picks, usable, q2, do2, kv.reshape(2, total_blocks, BLK, width))

    gk, gv = pl.pallas_call(
        functools.partial(reduce_kernel, n),
        out_shape=(jax.ShapeDtypeStruct((tokens, width), bf16),) * 2,
        in_specs=[vmem()] * 2,
        out_specs=(vmem(), vmem()),
        scratch_shapes=[
            pltpu.VMEM((n, tokens, width), bf16),
            pltpu.VMEM((half, tokens, width), bf16),
            pltpu.VMEM((rest, tokens, width), bf16),
            pltpu.VMEM((half, tokens, width), bf16),
            pltpu.VMEM((rest, tokens, width), bf16),
            pltpu.VMEM((2, tokens, width), bf16),
            dma((half * SUB,)), dma((half * SUB,)),
            dma((rest * SUB,)), dma((rest * SUB,)),
            dma((n,)), dma((n,)),
            dma((SUB,)), dma((SUB,)),
        ],
        compiler_params=pltpu.CompilerParams(
            collective_id=2, has_side_effects=True, vmem_limit_bytes=60 * 2**20
        ),
    )(mine.reshape(n, tokens, width), theirs.reshape(n, tokens, width))
    return (
        dq.reshape(tokens, 1, heads_here, width),
        gk.reshape(tokens, 1, width),
        gv.reshape(tokens, 1, width),
    )


def solution(mesh):
    return jax.shard_map(
        per_device,
        mesh=mesh,
        in_specs=(
            P(("groups", "seq"), "head", "inner", None),
            P(("groups", "seq"), "head", "inner", None),
            P(("groups", "seq"), "head", None),
            P(("groups", "seq"), "head", None),
            P("head", "groups", None),
            P("head", "groups", None),
        ),
        out_specs=(
            P(("groups", "seq"), "head", "inner", None),
            P(("groups", "seq"), "head", None),
            P(("groups", "seq"), "head", None),
        ),
        check_vma=False,
    )
```

time: 341 us -> 139 us (0.41)
  waiting for transfers between devices: 146 us -> 0 us
  Pallas kernels: 0 us -> 133 us
  other arithmetic: 56.3 us -> 0 us
  local copies, waits for them, and re-layouts: 54 us -> 5.25 us
  matrix products: 36.8 us -> 0 us
  blocking collectives: 24.7 us -> 0 us
  between operations: 14.4 us -> 0.65 us
  starting transfers between devices: 7.28 us -> 0 us
    pallas_call x0 -> x3, Pallas kernels: none -> 133 us  [the longest x1 76.6 us: per_device(): pl.pallas_call(functools.partial(gather_kernel, n), out_shape=jax.ShapeDt...]
    all_gather x1 -> x0, waiting for transfers between devices: 102 us -> none  [sent_together(): result, at, outs = (lax.all_gather(both, axis, axis=dim, tiled=True), 0, [])]
    all_to_all x1 -> x0, waiting for transfers between devices: 44.2 us -> none  [in_one_piece_2(): lax.all_to_all(both, axis, split_axis=split_dim, concat_axis=concat_dim,...]
    dot_general x22 -> x0, matrix products: 36.8 us -> none  [the longest x4 9.92 us: attend(): jnp.einsum('qigw,qsw->qgis', do_group, v_group, preferred_element_type=jn...]
    scatter-add x8 -> x0, other arithmetic: 29.9 us -> none  [the longest x4 19.2 us: attend(): key_acc.at[rows_group].add(key_terms.reshape(group * TOPK, BLK * width))]
    all_to_all x2 -> x0, blocking collectives: 24.7 us -> none  [the longest x1 15.2 us: summed_on_arrival(): parts = lax.all_to_all(cut_along(x, dim, size), axis, 0, 0, tiled=True)]
    reshape x10 -> x0, local copies, waits for them, and re-layouts: 12.1 us -> none  [the longest x4 5.66 us: attend(): value_terms.reshape(group * TOPK, BLK * width)]
    reduce_sum x3 -> x0, other arithmetic: 7.51 us -> none  [the longest x1 5.28 us: summed_on_arrival(): return jnp.sum(parts.astype(jnp.float32), axis=0)]
  transfers between devices with their start and end apart: 2 -> 0, of which waited for: 2 -> 0; matrix products, arithmetic and copies ran while one was open for 2% -> 0% of each run, Pallas kernels for 0% -> 0%
where the time goes in v1:
time: 139 us
  Pallas kernels  133 us (96%)
  local copies, waits for them, and re-layouts  5.25 us (4%)
    pallas_call x1, Pallas kernels, per_device(): pl.pallas_call(functools.partial(gather_kernel, n), out_shape=jax.ShapeDt...  76.6 us
    pallas_call x1, Pallas kernels, per_device(): pl.pallas_call(functools.partial(reduce_kernel, n), out_shape=(jax.ShapeD...  38.2 us
    pallas_call x1, Pallas kernels, per_device(): pl.pallas_call(functools.partial(attend_kernel, scaling), out_shape=(jax....  18 us
    unnamed x4, local copies, waits for them, and re-layouts  4.46 us

profile of v1, /device:TPU:65, one launch (start us, length us, event | category | flops | bytes accessed | tf_op | source)
XLA Modules:
  0.0 138.7 jit_solution(10785819378880443761)
XLA Ops:
  0.6 0.8 constant_dynamic-slice_fusion
  1.4 0.7 copy.13
  2.1 0.7 copy.12
  2.7 76.6 %shard_map.85 = bf16[2,16,512,128]{3,2,1,0:T(8,128)(2,1)} custom-call(bf16[512,128]{1,0:T(8,128)(2,1)} %bitcast.19, bf16[512,128]{1,0:T(8,128)(2,1)} %bitcast.20), custom_call_target="tpu_custom_call" | custom-call | tf_op jit(solution)/shard_map/pallas_call | solution.py:260
  79.3 18.0 %shard_map.86 = (bf16[2048,128]{1,0:T(8,128)(2,1)}, f32[128,64,128]{2,1,0:T(8,128)}, bf16[128,64,128]{2,1,0:T(8,128)(2,1)}) custom-call(s32[8,16]{1,0:T(8,128)} %bitcast.24, s32[8,16]{1,0:T(8,128)} %bitcast.23, bf16[2048,128]{1,0:T(8,128)(2,1)} %bitcast.17, bf16[2048,128]{1,0:T(8,128)(2,1)} %bitcast.18, bf16[2,128,64,128]{3,2,1,0:T(8,128)(2,1)} %bitcast.14), custom_call_target="tpu_custom_call" | custom-call | tf_op jit(solution)/shard_map/pallas_call | solution.py:277
  97.3 38.2 %shard_map.87 = (bf16[512,128]{1,0:T(8,128)(2,1)}, bf16[512,128]{1,0:T(8,128)(2,1)}) custom-call(f32[16,512,128]{2,1,0:T(8,128)} %bitcast.15, bf16[16,512,128]{2,1,0:T(8,128)(2,1)} %bitcast.16), custom_call_target="tpu_custom_call" | custom-call | tf_op jit(solution)/shard_map/pallas_call | solution.py:304
  135.5 1.6 %copy.16 = bf16[512,1,128]{2,0,1:T(8,128)(2,1)} copy(bf16[512,1,128]{2,0,1:T(8,128)(2,1)} %bitcast.22) | data formatting | bytes 262144
  137.1 1.6 %copy.17 = bf16[512,1,128]{2,0,1:T(8,128)(2,1)} copy(bf16[512,1,128]{2,0,1:T(8,128)(2,1)} %bitcast.21) | data formatting | bytes 262144

commit v2 on v1

v2 whole, which is shorter than its diff:
```python
import functools
import math

import jax
import jax.numpy as jnp
from jax import lax
from jax.experimental import pallas as pl
from jax.experimental.pallas import tpu as pltpu
from jax.sharding import PartitionSpec as P

BLK = 64
TOPK = 16
SUB = 4
MESH = pl.DeviceIdType.MESH
LOG2E = 1.4426950408889634


def places(n):
    me = lax.axis_index("seq")
    core = lax.axis_index("inner")
    up = {"seq": lax.rem(me + 1, n)}
    down = {"seq": lax.rem(me + n - 1, n)}
    partner = {"inner": 1 - core}
    return me, core, up, down, partner


def greet(n, me, up, down, partner):
    barrier = pltpu.get_barrier_semaphore()
    pl.semaphore_signal(barrier, inc=1, device_id=down, device_id_type=MESH)
    pl.semaphore_signal(barrier, inc=1, device_id=partner, device_id_type=MESH)

    @pl.when(me < n - 1)
    def _():
        pl.semaphore_signal(barrier, inc=1, device_id=up, device_id_type=MESH)

    pl.semaphore_wait(barrier, jnp.where(me > 0, 3, 2))


def send(src, dst, s_sem, r_sem, where):
    return pltpu.make_async_remote_copy(
        src_ref=src, dst_ref=dst, send_sem=s_sem, recv_sem=r_sem, device_id=where, device_id_type=MESH
    )


def gather_kernel(n, k_ref, v_ref, kv_ref, local_sem, us, ur, ws, wr, ps, pr, ready):
    me, core, up, down, partner = places(n)
    rows = k_ref.shape[0]
    part = rows // SUB
    half = n // 2
    wraps = n - 1 - half
    last = n - 1
    own_k = pltpu.make_async_copy(k_ref, kv_ref.at[0, me], local_sem.at[0])
    own_v = pltpu.make_async_copy(v_ref, kv_ref.at[1, me], local_sem.at[1])
    own_k.start()
    own_v.start()
    greet(n, me, up, down, partner)

    @pl.when(me == last)
    def _():
        pl.semaphore_signal(ready, inc=1, device_id=up, device_id_type=MESH)

    own_k.wait()
    own_v.wait()

    def piece(run, u):
        return kv_ref.at[core, run, pl.ds(u * part, part)]

    def up_copy(run, u):
        return send(piece(run, u), piece(run, u), us.at[run, u], ur.at[run, u], up)

    def wrap_copy(run, u):
        return send(piece(run, u), piece(run, u), ws.at[run, u], wr.at[run, u], down)

    def share_copy(run):
        return send(kv_ref.at[core, run], kv_ref.at[core, run], ps.at[run], pr.at[run], partner)

    @pl.when(me < last)
    def _():
        for u in range(SUB):
            up_copy(me, u).start()

    @pl.when(me == 0)
    def _():
        pl.semaphore_wait(ready, 1)

    lag = jnp.where(me > half, (5 * (last - me) + 2) // 3, 0)
    for j in range(wraps + half - 2 + 2):
        if j < half:
            run = me - 1 - j

            @pl.when(run >= 0)
            def _():
                for u in range(SUB):
                    up_copy(run, u).wait_recv()
                    if j + 1 < half:

                        @pl.when(me < last)
                        def _():
                            up_copy(run, u).start()

                share_copy(run).start()

        w = j - lag
        low = (me <= w) & (w < wraps)

        @pl.when(low)
        def _():
            for u in range(SUB):

                @pl.when(w > me)
                def _():
                    wrap_copy(w, u).wait_recv()

                wrap_copy(w, u).start()

        @pl.when((w >= 0) & (w + half < me))
        def _():
            for u in range(SUB):
                wrap_copy(w, u).wait_recv()

                @pl.when(w + half + 1 < me)
                def _():
                    wrap_copy(w, u).start()

            share_copy(w).start()

    for run in range(n - 1):

        @pl.when(run < me)
        def _():
            share_copy(run).wait_recv()
            share_copy(run).wait_send()

        @pl.when((run <= me) & (me < min(run + half, last)))
        def _():
            for u in range(SUB):
                up_copy(run, u).wait_send()

        if run < wraps:

            @pl.when((me <= run) | (me > run + half + 1))
            def _():
                for u in range(SUB):
                    wrap_copy(run, u).wait_send()


def attend_kernel(scaling, picks, usable, q_ref, do_ref, kv_ref, dq_ref, tiles_ref, acc):
    i = pl.program_id(0)
    at = lax.axis_index("seq") * pl.num_programs(0) + i
    rows = q_ref.shape[0]
    per_pos = rows // BLK

    @pl.when(i == 0)
    def _():
        acc[...] = jnp.zeros_like(acc)

    q = q_ref[...]
    do = do_ref[...]
    names = [jnp.where(usable[t, at] > 0, picks[t, at], at) for t in range(TOPK)]
    ks = jnp.concatenate([kv_ref[0, b] for b in names], axis=0)
    vs = jnp.concatenate([kv_ref[1, b] for b in names], axis=0)
    nt = (((1,), (1,)), ((), ()))
    st = lax.dot_general(ks, q, nt, preferred_element_type=jnp.float32)
    key_at = lax.broadcasted_iota(jnp.int32, (BLK, rows), 0)
    query_at = lax.broadcasted_iota(jnp.int32, (BLK, rows), 1) // per_pos
    low = jnp.float32(-1e30)
    parts = [jnp.where(key_at <= query_at, st[:BLK], low)]
    for t in range(1, TOPK):
        bias = jnp.where(usable[t, at] > 0, jnp.float32(0.0), low)
        parts.append(st[t * BLK : (t + 1) * BLK] + bias)
    st = jnp.concatenate(parts, axis=0)
    top = jnp.max(st, axis=0, keepdims=True)
    w = jnp.exp2((st - top) * jnp.float32(scaling * LOG2E))
    inv = 1.0 / jnp.sum(w, axis=0, keepdims=True)
    p = w * inv
    dp = lax.dot_general(vs, do, nt, preferred_element_type=jnp.float32)
    delta = jnp.sum(p * dp, axis=0, keepdims=True)
    dsc = (p * (dp - delta)).astype(jnp.bfloat16)
    pb = p.astype(jnp.bfloat16)
    dqt = lax.dot_general(ks, dsc, (((0,), (0,)), ((), ())), preferred_element_type=jnp.float32)
    dq_ref[...] = (dqt.T * scaling).astype(jnp.bfloat16)
    dk = jnp.dot(dsc, q, preferred_element_type=jnp.float32) * scaling
    dv = jnp.dot(pb, do, preferred_element_type=jnp.float32)
    for t in range(TOPK):
        acc[0, names[t]] += dk[t * BLK : (t + 1) * BLK]
        acc[1, names[t]] += dv[t * BLK : (t + 1) * BLK]

    @pl.when(i == pl.num_programs(0) - 1)
    def _():
        tiles_ref[...] = acc[...].astype(jnp.bfloat16)


def reduce_kernel(
    n, tiles, out, peer, got_down, got_up, put_down, put_up, final, ds, dr, us, ur, ps, pr, fs, fr
):
    me, core, up, down, partner = places(n)
    rows = tiles.shape[2]
    part = rows // SUB
    half = n // 2
    wraps = n - 1 - half
    last = n - 1
    greet(n, me, up, down, partner)

    def hand(run):
        return send(tiles.at[1 - core, run], peer.at[run], ps.at[run], pr.at[run], partner)

    for t in range(half):
        for run in (me - half + t, me - half - 1 - t):

            @pl.when(run >= 0)
            def _():
                hand(run).start()

    hand(me).start()

    def base(run, u):
        s = pl.ds(u * part, part)
        return tiles[core, run, s, :].astype(jnp.float32) + peer[run, s, :].astype(jnp.float32)

    def down_copy(run, u):
        s = pl.ds(u * part, part)
        return send(put_down.at[run, s], got_down.at[run, s], ds.at[run, u], dr.at[run, u], down)

    def up_copy(run, u, put):
        s = pl.ds(u * part, part)
        return send(put.at[run, s], got_up.at[run, s], us.at[run, u], ur.at[run, u], up)

    for t in range(half):
        wrap = me - half - 1 - t
        run = me - half + t

        @pl.when(wrap >= 0)
        def _():
            hand(wrap).wait_recv()
            for u in range(SUB):
                s = pl.ds(u * part, part)
                val = base(wrap, u)
                if t > 0:
                    up_copy(wrap, u, put_up).wait_recv()
                    val = val + got_up[wrap, s, :].astype(jnp.float32)
                put_up[wrap, s, :] = val.astype(jnp.bfloat16)
                up_copy(wrap, u, put_up).start()

        @pl.when(run >= 0)
        def _():
            hand(run).wait_recv()
            for u in range(SUB):
                s = pl.ds(u * part, part)
                if t == 0:
                    put_down[run, s, :] = base(run, u).astype(jnp.bfloat16)
                else:

                    @pl.when(me < last)
                    def _():
                        down_copy(run, u).wait_recv()
                        val = base(run, u) + got_down[run, s, :].astype(jnp.float32)
                        put_down[run, s, :] = val.astype(jnp.bfloat16)

                    @pl.when(me == last)
                    def _():
                        put_down[run, s, :] = base(run, u).astype(jnp.bfloat16)

                down_copy(run, u).start()

    for o in range(wraps - 1, 0, -1):

        @pl.when(me < o)
        def _():
            for u in range(SUB):
                up_copy(o, u, got_up).wait_recv()
                up_copy(o, u, got_up).start()

    hand(me).wait_recv()
    for u in range(SUB):
        s = pl.ds(u * part, part)

        @pl.when(me < last)
        def _():
            down_copy(me, u).wait_recv()

        @pl.when(me < wraps)
        def _():
            up_copy(me, u, got_up).wait_recv()
            final[core, s, :] = (
                base(me, u)
                + got_down[me, s, :].astype(jnp.float32)
                + got_up[me, s, :].astype(jnp.float32)
            ).astype(jnp.bfloat16)

        @pl.when((me >= wraps) & (me < last))
        def _():
            val = base(me, u) + got_down[me, s, :].astype(jnp.float32)
            final[core, s, :] = val.astype(jnp.bfloat16)

        @pl.when(me == last)
        def _():
            final[core, s, :] = base(me, u).astype(jnp.bfloat16)

        send(final.at[core, s], final.at[core, s], fs.at[u], fr.at[u], partner).start()
    for u in range(SUB):
        s = pl.ds(u * part, part)
        send(final.at[core, s], final.at[core, s], fs.at[u], fr.at[u], partner).wait()
    for run in range(n):

        @pl.when(run <= me)
        def _():
            hand(run).wait_send()

        @pl.when((run < me) & (me <= run + half))
        def _():
            for u in range(SUB):
                down_copy(run, u).wait_send()

        if run < wraps:

            @pl.when((me < run) | (me > run + half))
            def _():
                for u in range(SUB):
                    up_copy(run, u, got_up).wait_send()

    out[...] = final[...]


def vmem():
    return pl.BlockSpec(memory_space=pltpu.VMEM)


def anywhere():
    return pl.BlockSpec(memory_space=pl.ANY)


def per_device(queries, grad_out, keys, values, indices, valid):
    tokens, _, heads_here, width = queries.shape
    n = lax.axis_size("seq")
    blocks = tokens // BLK
    total_blocks = n * blocks
    scaling = 1.0 / math.sqrt(width)
    rows = BLK * heads_here
    half = n // 2
    rest = n - 1 - half
    dma = pltpu.SemaphoreType.DMA
    bf16, f32 = jnp.bfloat16, jnp.float32
    picks, usable = indices[0].T, valid[0].T

    kv = pl.pallas_call(
        functools.partial(gather_kernel, n),
        out_shape=jax.ShapeDtypeStruct((2, n, tokens, width), bf16),
        in_specs=[anywhere()] * 2,
        out_specs=vmem(),
        scratch_shapes=[
            dma((2,)),
            dma((n, SUB)), dma((n, SUB)),
            dma((rest, SUB)), dma((rest, SUB)),
            dma((n,)), dma((n,)),
            pltpu.SemaphoreType.REGULAR,
        ],
        compiler_params=pltpu.CompilerParams(collective_id=1, has_side_effects=True),
    )(keys[:, 0], values[:, 0])

    q2 = queries.reshape(tokens * heads_here, width)
    do2 = grad_out.reshape(tokens * heads_here, width)
    full = (2, total_blocks, BLK, width)
    whole = lambda i, *_: (0, 0, 0, 0)
    by_block = pl.BlockSpec((rows, width), lambda i, *_: (i, 0))
    dq, tiles = pl.pallas_call(
        functools.partial(attend_kernel, scaling),
        out_shape=(
            jax.ShapeDtypeStruct((tokens * heads_here, width), bf16),
            jax.ShapeDtypeStruct(full, bf16),
        ),
        grid_spec=pltpu.PrefetchScalarGridSpec(
            num_scalar_prefetch=2,
            grid=(blocks,),
            in_specs=[by_block, by_block, pl.BlockSpec(full, whole)],
            out_specs=[by_block, pl.BlockSpec(full, whole)],
            scratch_shapes=[pltpu.VMEM(full, f32)],
        ),
        compiler_params=pltpu.CompilerParams(
            dimension_semantics=("arbitrary",), vmem_limit_bytes=60 * 2**20
        ),
    )(picks, usable, q2, do2, kv.reshape(full))

    own = pl.pallas_call(
        functools.partial(reduce_kernel, n),
        out_shape=jax.ShapeDtypeStruct((2, tokens, width), bf16),
        in_specs=[vmem()],
        out_specs=vmem(),
        scratch_shapes=[
            pltpu.VMEM((n, tokens, width), bf16),
            pltpu.VMEM((n, tokens, width), bf16),
            pltpu.VMEM((rest, tokens, width), bf16),
            pltpu.VMEM((n, tokens, width), bf16),
            pltpu.VMEM((rest, tokens, width), bf16),
            pltpu.VMEM((2, tokens, width), bf16),
            dma((n, SUB)), dma((n, SUB)),
            dma((rest, SUB)), dma((rest, SUB)),
            dma((n,)), dma((n,)),
            dma((SUB,)), dma((SUB,)),
        ],
        compiler_params=pltpu.CompilerParams(
            collective_id=2, has_side_effects=True, vmem_limit_bytes=60 * 2**20
        ),
    )(tiles.reshape(2, n, tokens, width))
    gk, gv = own[0], own[1]
    return (
        dq.reshape(tokens, 1, heads_here, width),
        gk.reshape(tokens, 1, width),
        gv.reshape(tokens, 1, width),
    )


def solution(mesh):
    return jax.shard_map(
        per_device,
        mesh=mesh,
        in_specs=(
            P(("groups", "seq"), "head", "inner", None),
            P(("groups", "seq"), "head", "inner", None),
            P(("groups", "seq"), "head", None),
            P(("groups", "seq"), "head", None),
            P("head", "groups", None),
            P("head", "groups", None),
        ),
        out_specs=(
            P(("groups", "seq"), "head", "inner", None),
            P(("groups", "seq"), "head", None),
            P(("groups", "seq"), "head", None),
        ),
        check_vma=False,
    )
```

time: 139 us -> 143 us (1.029)
  Pallas kernels: 133 us -> 140 us
  local copies, waits for them, and re-layouts: 5.25 us -> 1.69 us
    pallas_call x1, Pallas kernels: 76.6 us -> 81.5 us  [per_device(): pl.pallas_call(functools.partial(gather_kernel, n), out_shape=jax.ShapeDt...]
    unnamed x4 -> x0, local copies, waits for them, and re-layouts: 4.46 us -> none
    pallas_call x1, Pallas kernels: 38.2 us -> 41 us  [per_device(): pl.pallas_call(functools.partial(reduce_kernel, n), out_shape=jax.ShapeDt...]
    another operation x0 -> x1, local copies, waits for them, and re-layouts: none -> 1.69 us  [per_device(): gv.reshape(tokens, 1, width)]
where the time goes in v2:
time: 143 us; the launch traced here: 142 us
  Pallas kernels  140 us (98%)
  local copies, waits for them, and re-layouts  1.69 us (1%)
    pallas_call x1, Pallas kernels, per_device(): pl.pallas_call(functools.partial(gather_kernel, n), out_shape=jax.ShapeDt...  81.5 us
    pallas_call x1, Pallas kernels, per_device(): pl.pallas_call(functools.partial(reduce_kernel, n), out_shape=jax.ShapeDt...  41 us
    pallas_call x1, Pallas kernels, per_device(): pl.pallas_call(functools.partial(attend_kernel, scaling), out_shape=(jax....  17.5 us

profile of v2, /device:TPU:65, one launch (start us, length us, event | category | flops | bytes accessed | tf_op | source)
XLA Modules:
  0.0 142.4 jit_solution(15102374930562212878)
XLA Ops:
  0.6 81.5 %shard_map.85 = bf16[2,16,512,128]{3,2,1,0:T(8,128)(2,1)} custom-call(bf16[512,128]{1,0:T(8,128)(2,1)} %bitcast.23, bf16[512,128]{1,0:T(8,128)(2,1)} %bitcast.24), custom_call_target="tpu_custom_call" | custom-call | tf_op jit(solution)/shard_map/pallas_call | solution.py:345
  82.1 17.5 %shard_map.86 = (bf16[2048,128]{1,0:T(8,128)(2,1)}, bf16[2,128,64,128]{3,2,1,0:T(8,128)(2,1)}) custom-call(s32[16,128]{1,0:T(8,128)} %bitcast.25, s32[16,128]{1,0:T(8,128)} %bitcast.26, bf16[2048,128]{1,0:T(8,128)(2,1)} %bitcast.21, bf16[2048,128]{1,0:T(8,128)(2,1)} %bitcast.22, bf16[2,128,64,128]{3,2,1,0:T(8,128)(2,1)} %bitcast.19), custom_call_target="tpu_custom_call" | custom-call | tf_op jit(solution)/shard_map/pallas_call | solution.py:365
  99.6 41.0 %shard_map.87 = bf16[2,512,128]{2,1,0:T(8,128)(2,1)} custom-call(bf16[2,16,512,128]{3,2,1,0:T(8,128)(2,1)} %bitcast.20), custom_call_target="tpu_custom_call" | custom-call | tf_op jit(solution)/shard_map/pallas_call | solution.py:383
  140.7 1.7 %slice_bitcast_fusion = (bf16[512,1,128]{2,0,1:T(8,128)(2,1)}, bf16[512,1,128]{2,0,1:T(8,128)(2,1)}) fusion(bf16[2,512,128]{2,1,0:T(8,128)(2,1)} %shard_map.87), kind=kLoop, calls=%fused_computation | loop fusion | bytes 524288 | tf_op jit(solution)/shard_map/reshape;squeeze | solution.py:408

commit v3 on v2

--- a/solution.py
+++ b/solution.py
@@ -24,16 +24,19 @@
     return me, core, up, down, partner
 
 
-def greet(n, me, up, down, partner):
+def meet(signals, count):
     barrier = pltpu.get_barrier_semaphore()
-    pl.semaphore_signal(barrier, inc=1, device_id=down, device_id_type=MESH)
-    pl.semaphore_signal(barrier, inc=1, device_id=partner, device_id_type=MESH)
-
-    @pl.when(me < n - 1)
-    def _():
-        pl.semaphore_signal(barrier, inc=1, device_id=up, device_id_type=MESH)
-
-    pl.semaphore_wait(barrier, jnp.where(me > 0, 3, 2))
+    for needed, where in signals:
+
+        @pl.when(needed)
+        def _():
+            pl.semaphore_signal(barrier, inc=1, device_id=where, device_id_type=MESH)
+
+    pl.semaphore_wait(barrier, count)
+
+
+def one_if(cond):
+    return jnp.where(cond, 1, 0)
 
 
 def send(src, dst, s_sem, r_sem, where):
@@ -53,11 +56,21 @@
     own_v = pltpu.make_async_copy(v_ref, kv_ref.at[1, me], local_sem.at[1])
     own_k.start()
     own_v.start()
-    greet(n, me, up, down, partner)
+    far = {"seq": last}
+    meet(
+        (
+            (me > 0, partner),
+            (me > 0, down),
+            ((me > half) & (me < last), up),
+            (me < wraps, far),
+        ),
+        one_if(me > 0) + one_if(me < last) + one_if(me > half + 1) + jnp.where(me == last, wraps, 0),
+    )
 
     @pl.when(me == last)
     def _():
-        pl.semaphore_signal(ready, inc=1, device_id=up, device_id_type=MESH)
+        for s in range(wraps):
+            pl.semaphore_signal(ready, inc=1, device_id={"seq": s}, device_id_type=MESH)
 
     own_k.wait()
     own_v.wait()
@@ -79,14 +92,23 @@
         for u in range(SUB):
             up_copy(me, u).start()
 
+    def own_wrap():
+        pl.semaphore_wait(ready, 1)
+        for u in range(SUB):
+            send(piece(me, u), piece(me, u), ws.at[me, u], wr.at[me, u], far).start()
+
     @pl.when(me == 0)
     def _():
-        pl.semaphore_wait(ready, 1)
-
-    lag = jnp.where(me > half, (5 * (last - me) + 2) // 3, 0)
-    for j in range(wraps + half - 2 + 2):
+        own_wrap()
+
+    lag = (5 * (last - me) + 2) // 3
+    for j in range(wraps + half - 2):
         if j < half:
             run = me - 1 - j
+
+            @pl.when((run == 0) & (me > half // 2) & (me < wraps))
+            def _():
+                own_wrap()
 
             @pl.when(run >= 0)
             def _():
@@ -100,19 +122,11 @@
 
                 share_copy(run).start()
 
+            @pl.when((run == 0) & (me <= half // 2))
+            def _():
+                own_wrap()
+
         w = j - lag
-        low = (me <= w) & (w < wraps)
-
-        @pl.when(low)
-        def _():
-            for u in range(SUB):
-
-                @pl.when(w > me)
-                def _():
-                    wrap_copy(w, u).wait_recv()
-
-                wrap_copy(w, u).start()
-
         @pl.when((w >= 0) & (w + half < me))
         def _():
             for u in range(SUB):
@@ -138,7 +152,7 @@
 
         if run < wraps:
 
-            @pl.when((me <= run) | (me > run + half + 1))
+            @pl.when((me == run) | (me > run + half + 1))
             def _():
                 for u in range(SUB):
                     wrap_copy(run, u).wait_send()
@@ -199,7 +213,16 @@
     half = n // 2
     wraps = n - 1 - half
     last = n - 1
-    greet(n, me, up, down, partner)
+    far = {"seq": last}
+    meet(
+        (
+            (me >= 0, partner),
+            (me < last, up),
+            (me > half + 1, down),
+            (me < wraps, far),
+        ),
+        1 + one_if(me > 0) + one_if((me > half) & (me < last)) + jnp.where(me == last, wraps, 0),
+    )
 
     def hand(run):
         return send(tiles.at[1 - core, run], peer.at[run], ps.at[run], pr.at[run], partner)
@@ -221,9 +244,10 @@
         s = pl.ds(u * part, part)
         return send(put_down.at[run, s], got_down.at[run, s], ds.at[run, u], dr.at[run, u], down)
 
-    def up_copy(run, u, put):
+    def up_copy(run, u):
         s = pl.ds(u * part, part)
-        return send(put.at[run, s], got_up.at[run, s], us.at[run, u], ur.at[run, u], up)
+        where = {"seq": jnp.where(me == last, run, lax.rem(me + 1, n))}
+        return send(put_up.at[run, s], got_up.at[run, s], us.at[run, u], ur.at[run, u], where)
 
     for t in range(half):
         wrap = me - half - 1 - t
@@ -236,10 +260,10 @@
                 s = pl.ds(u * part, part)
                 val = base(wrap, u)
                 if t > 0:
-                    up_copy(wrap, u, put_up).wait_recv()
+                    up_copy(wrap, u).wait_recv()
                     val = val + got_up[wrap, s, :].astype(jnp.float32)
                 put_up[wrap, s, :] = val.astype(jnp.bfloat16)
-                up_copy(wrap, u, put_up).start()
+                up_copy(wrap, u).start()
 
         @pl.when(run >= 0)
         def _():
@@ -262,14 +286,6 @@
 
                 down_copy(run, u).start()
 
-    for o in range(wraps - 1, 0, -1):
-
-        @pl.when(me < o)
-        def _():
-            for u in range(SUB):
-                up_copy(o, u, got_up).wait_recv()
-                up_copy(o, u, got_up).start()
-
     hand(me).wait_recv()
     for u in range(SUB):
         s = pl.ds(u * part, part)
@@ -280,7 +296,7 @@
 
         @pl.when(me < wraps)
         def _():
-            up_copy(me, u, got_up).wait_recv()
+            up_copy(me, u).wait_recv()
             final[core, s, :] = (
                 base(me, u)
                 + got_down[me, s, :].astype(jnp.float32)
@@ -313,10 +329,10 @@
 
         if run < wraps:
 
-            @pl.when((me < run) | (me > run + half))
+            @pl.when(me > run + half)
             def _():
                 for u in range(SUB):
-                    up_copy(run, u, got_up).wait_send()
+                    up_copy(run, u).wait_send()
 
     out[...] = final[...]
 

time: 143 us -> 145 us (1.014)
  Pallas kernels: 140 us -> 142 us
    pallas_call x1, Pallas kernels: 41 us -> 57.6 us  [per_device(): pl.pallas_call(functools.partial(reduce_kernel, n), out_shape=jax.ShapeDt...]
    pallas_call x1, Pallas kernels: 81.5 us -> 66.9 us  [per_device(): pl.pallas_call(functools.partial(gather_kernel, n), out_shape=jax.ShapeDt...]
where the time goes in v3:
time: 145 us; the launch traced here: 144 us
  Pallas kernels  142 us (98%)
  local copies, waits for them, and re-layouts  1.69 us (1%)
    pallas_call x1, Pallas kernels, per_device(): pl.pallas_call(functools.partial(gather_kernel, n), out_shape=jax.ShapeDt...  66.9 us
    pallas_call x1, Pallas kernels, per_device(): pl.pallas_call(functools.partial(reduce_kernel, n), out_shape=jax.ShapeDt...  57.6 us
    pallas_call x1, Pallas kernels, per_device(): pl.pallas_call(functools.partial(attend_kernel, scaling), out_shape=(jax....  17.5 us

profile of v3, /device:TPU:65, one launch (start us, length us, event | category | flops | bytes accessed | tf_op | source)
XLA Modules:
  0.0 144.3 jit_solution(7880458644217785009)
XLA Ops:
  0.6 66.9 %shard_map.85 = bf16[2,16,512,128]{3,2,1,0:T(8,128)(2,1)} custom-call(bf16[512,128]{1,0:T(8,128)(2,1)} %bitcast.23, bf16[512,128]{1,0:T(8,128)(2,1)} %bitcast.24), custom_call_target="tpu_custom_call" | custom-call | tf_op jit(solution)/shard_map/pallas_call | solution.py:361
  67.6 17.5 %shard_map.86 = (bf16[2048,128]{1,0:T(8,128)(2,1)}, bf16[2,128,64,128]{3,2,1,0:T(8,128)(2,1)}) custom-call(s32[16,128]{1,0:T(8,128)} %bitcast.25, s32[16,128]{1,0:T(8,128)} %bitcast.26, bf16[2048,128]{1,0:T(8,128)(2,1)} %bitcast.21, bf16[2048,128]{1,0:T(8,128)(2,1)} %bitcast.22, bf16[2,128,64,128]{3,2,1,0:T(8,128)(2,1)} %bitcast.19), custom_call_target="tpu_custom_call" | custom-call | tf_op jit(solution)/shard_map/pallas_call | solution.py:381
  85.1 57.6 %shard_map.87 = bf16[2,512,128]{2,1,0:T(8,128)(2,1)} custom-call(bf16[2,16,512,128]{3,2,1,0:T(8,128)(2,1)} %bitcast.20), custom_call_target="tpu_custom_call" | custom-call | tf_op jit(solution)/shard_map/pallas_call | solution.py:399
  142.7 1.7 %slice_bitcast_fusion = (bf16[512,1,128]{2,0,1:T(8,128)(2,1)}, bf16[512,1,128]{2,0,1:T(8,128)(2,1)}) fusion(bf16[2,512,128]{2,1,0:T(8,128)(2,1)} %shard_map.87), kind=kLoop, calls=%fused_computation | loop fusion | bytes 524288 | tf_op jit(solution)/shard_map/reshape;squeeze | solution.py:424

commit v4 on v2

--- a/solution.py
+++ b/solution.py
@@ -79,15 +79,38 @@
         for u in range(SUB):
             up_copy(me, u).start()
 
+    def pass_on(w):
+        for u in range(SUB):
+
+            @pl.when(w > me)
+            def _():
+                wrap_copy(w, u).wait_recv()
+
+            wrap_copy(w, u).start()
+
     @pl.when(me == 0)
     def _():
         pl.semaphore_wait(ready, 1)
 
-    lag = jnp.where(me > half, (5 * (last - me) + 2) // 3, 0)
+    for w in range(wraps):
+
+        @pl.when((me == 0) | (me == w))
+        def _():
+            pass_on(w)
+
+    lag = (5 * (last - me) + 2) // 3
     for j in range(wraps + half - 2 + 2):
         if j < half:
             run = me - 1 - j
 
+            @pl.when(run == 0)
+            def _():
+                for w in range(1, wraps):
+
+                    @pl.when(w > me)
+                    def _():
+                        pass_on(w)
+
             @pl.when(run >= 0)
             def _():
                 for u in range(SUB):
@@ -101,18 +124,6 @@
                 share_copy(run).start()
 
         w = j - lag
-        low = (me <= w) & (w < wraps)
-
-        @pl.when(low)
-        def _():
-            for u in range(SUB):
-
-                @pl.when(w > me)
-                def _():
-                    wrap_copy(w, u).wait_recv()
-
-                wrap_copy(w, u).start()
-
         @pl.when((w >= 0) & (w + half < me))
         def _():
             for u in range(SUB):
@@ -144,7 +155,9 @@
                     wrap_copy(run, u).wait_send()
 
 
-def attend_kernel(scaling, picks, usable, q_ref, do_ref, kv_ref, dq_ref, tiles_ref, acc):
+def attend_kernel(
+    scaling, n, picks, usable, q_ref, do_ref, kv_hbm, dq_ref, tiles_ref, acc, kv_ref, stage, in_sem, out_sem
+):
     i = pl.program_id(0)
     at = lax.axis_index("seq") * pl.num_programs(0) + i
     rows = q_ref.shape[0]
@@ -152,7 +165,10 @@
 
     @pl.when(i == 0)
     def _():
+        load = pltpu.make_async_copy(kv_hbm, kv_ref, in_sem)
+        load.start()
         acc[...] = jnp.zeros_like(acc)
+        load.wait()
 
     q = q_ref[...]
     do = do_ref[...]
@@ -187,11 +203,20 @@
 
     @pl.when(i == pl.num_programs(0) - 1)
     def _():
-        tiles_ref[...] = acc[...].astype(jnp.bfloat16)
+        per_run = acc.shape[1] // n
+        outs = []
+        for r in range(n):
+            s = pl.ds(r * per_run, per_run)
+            stage[:, s] = acc[:, s].astype(jnp.bfloat16)
+            c = pltpu.make_async_copy(stage.at[:, s], tiles_ref.at[:, s], out_sem.at[r])
+            c.start()
+            outs.append(c)
+        for c in outs:
+            c.wait()
 
 
 def reduce_kernel(
-    n, tiles, out, peer, got_down, got_up, put_down, put_up, final, ds, dr, us, ur, ps, pr, fs, fr
+    n, tiles_hbm, out, tiles, ls, peer, got_down, got_up, put_down, put_up, final, ds, dr, us, ur, ps, pr, fs, fr
 ):
     me, core, up, down, partner = places(n)
     rows = tiles.shape[2]
@@ -199,18 +224,32 @@
     half = n // 2
     wraps = n - 1 - half
     last = n - 1
+
+    def load(run):
+        return pltpu.make_async_copy(tiles_hbm.at[:, run], tiles.at[:, run], ls.at[run])
+
+    for t in range(half):
+        for run in (me - half - 1 - t, me - half + t):
+
+            @pl.when(run >= 0)
+            def _():
+                load(run).start()
+
+    load(me).start()
     greet(n, me, up, down, partner)
 
     def hand(run):
         return send(tiles.at[1 - core, run], peer.at[run], ps.at[run], pr.at[run], partner)
 
     for t in range(half):
-        for run in (me - half + t, me - half - 1 - t):
+        for run in (me - half - 1 - t, me - half + t):
 
             @pl.when(run >= 0)
             def _():
+                load(run).wait()
                 hand(run).start()
 
+    load(me).wait()
     hand(me).start()
 
     def base(run, u):
@@ -360,10 +399,9 @@
     q2 = queries.reshape(tokens * heads_here, width)
     do2 = grad_out.reshape(tokens * heads_here, width)
     full = (2, total_blocks, BLK, width)
-    whole = lambda i, *_: (0, 0, 0, 0)
     by_block = pl.BlockSpec((rows, width), lambda i, *_: (i, 0))
     dq, tiles = pl.pallas_call(
-        functools.partial(attend_kernel, scaling),
+        functools.partial(attend_kernel, scaling, n),
         out_shape=(
             jax.ShapeDtypeStruct((tokens * heads_here, width), bf16),
             jax.ShapeDtypeStruct(full, bf16),
@@ -371,9 +409,15 @@
         grid_spec=pltpu.PrefetchScalarGridSpec(
             num_scalar_prefetch=2,
             grid=(blocks,),
-            in_specs=[by_block, by_block, pl.BlockSpec(full, whole)],
-            out_specs=[by_block, pl.BlockSpec(full, whole)],
-            scratch_shapes=[pltpu.VMEM(full, f32)],
+            in_specs=[by_block, by_block, anywhere()],
+            out_specs=[by_block, anywhere()],
+            scratch_shapes=[
+                pltpu.VMEM(full, f32),
+                pltpu.VMEM(full, bf16),
+                pltpu.VMEM(full, bf16),
+                dma,
+                dma((n,)),
+            ],
         ),
         compiler_params=pltpu.CompilerParams(
             dimension_semantics=("arbitrary",), vmem_limit_bytes=60 * 2**20
@@ -383,9 +427,11 @@
     own = pl.pallas_call(
         functools.partial(reduce_kernel, n),
         out_shape=jax.ShapeDtypeStruct((2, tokens, width), bf16),
-        in_specs=[vmem()],
+        in_specs=[anywhere()],
         out_specs=vmem(),
         scratch_shapes=[
+            pltpu.VMEM((2, n, tokens, width), bf16),
+            dma((n,)),
             pltpu.VMEM((n, tokens, width), bf16),
             pltpu.VMEM((n, tokens, width), bf16),
             pltpu.VMEM((rest, tokens, width), bf16),

time: 143 us -> 154 us (1.077)
  Pallas kernels: 140 us -> 152 us
    pallas_call x1, Pallas kernels: 41 us -> 69.7 us  [per_device(): pl.pallas_call(functools.partial(reduce_kernel, n), out_shape=jax.ShapeDt...]
    pallas_call x1, Pallas kernels: 81.5 us -> 63.9 us  [per_device(): pl.pallas_call(functools.partial(gather_kernel, n), out_shape=jax.ShapeDt...]
where the time goes in v4:
time: 154 us
  Pallas kernels  152 us (99%)
  local copies, waits for them, and re-layouts  1.69 us (1%)
    pallas_call x1, Pallas kernels, per_device(): pl.pallas_call(functools.partial(reduce_kernel, n), out_shape=jax.ShapeDt...  69.7 us
    pallas_call x1, Pallas kernels, per_device(): pl.pallas_call(functools.partial(gather_kernel, n), out_shape=jax.ShapeDt...  63.9 us
    pallas_call x1, Pallas kernels, per_device(): pl.pallas_call(functools.partial(attend_kernel, scaling, n), out_shape=(j...  18.2 us

profile of v4, /device:TPU:65, one launch (start us, length us, event | category | flops | bytes accessed | tf_op | source)
XLA Modules:
  0.0 154.1 jit_solution(17468027301797140125)
XLA Ops:
  0.6 63.9 %shard_map.85 = bf16[2,16,512,128]{3,2,1,0:T(8,128)(2,1)} custom-call(bf16[512,128]{1,0:T(8,128)(2,1)} %bitcast.23, bf16[512,128]{1,0:T(8,128)(2,1)} %bitcast.24), custom_call_target="tpu_custom_call" | custom-call | tf_op jit(solution)/shard_map/pallas_call | solution.py:384
  64.5 18.2 %shard_map.86 = (bf16[2048,128]{1,0:T(8,128)(2,1)}, bf16[2,128,64,128]{3,2,1,0:T(8,128)(2,1)}) custom-call(s32[16,128]{1,0:T(8,128)} %bitcast.25, s32[16,128]{1,0:T(8,128)} %bitcast.26, bf16[2048,128]{1,0:T(8,128)(2,1)} %bitcast.21, bf16[2048,128]{1,0:T(8,128)(2,1)} %bitcast.22, bf16[2,128,64,128]{3,2,1,0:T(8,128)(2,1)} %bitcast.19), custom_call_target="tpu_custom_call" | custom-call | tf_op jit(solution)/shard_map/pallas_call | solution.py:403
  82.7 69.7 %shard_map.87 = bf16[2,512,128]{2,1,0:T(8,128)(2,1)} custom-call(bf16[2,16,512,128]{3,2,1,0:T(8,128)(2,1)} %bitcast.20), custom_call_target="tpu_custom_call" | custom-call | tf_op jit(solution)/shard_map/pallas_call | solution.py:427
  152.4 1.7 %slice_bitcast_fusion = (bf16[512,1,128]{2,0,1:T(8,128)(2,1)}, bf16[512,1,128]{2,0,1:T(8,128)(2,1)}) fusion(bf16[2,512,128]{2,1,0:T(8,128)(2,1)} %shard_map.87), kind=kLoop, calls=%fused_computation | loop fusion | bytes 524288 | tf_op jit(solution)/shard_map/reshape;squeeze | solution.py:454

commit v5 on v2

v5 whole, which is shorter than its diff:
```python
import functools
import math

import jax
import jax.numpy as jnp
from jax import lax
from jax.experimental import pallas as pl
from jax.experimental.pallas import tpu as pltpu
from jax.sharding import PartitionSpec as P

BLK = 64
TOPK = 16
SUB = 4
MESH = pl.DeviceIdType.MESH
LOG2E = 1.4426950408889634


def greet(n):
    me = lax.axis_index("seq")
    core = lax.axis_index("inner")
    barrier = pltpu.get_barrier_semaphore()
    peers = ({"seq": lax.rem(me + 1, n)}, {"seq": lax.rem(me + n - 1, n)}, {"inner": 1 - core})
    for where in peers:
        pl.semaphore_signal(barrier, inc=1, device_id=where, device_id_type=MESH)
    pl.semaphore_wait(barrier, len(peers))


def send(src, dst, s_sem, r_sem, where):
    return pltpu.make_async_remote_copy(
        src_ref=src, dst_ref=dst, send_sem=s_sem, recv_sem=r_sem, device_id=where, device_id_type=MESH
    )


def gather_kernel(n, sub, k_ref, v_ref, kv_ref, local_sem, ss, rs, ps, pr):
    me = lax.axis_index("seq")
    core = lax.axis_index("inner")
    way = 1 - 2 * core
    ahead = {"seq": lax.rem(me + way + n, n)}
    partner = {"inner": 1 - core}
    part = k_ref.shape[0] // sub
    half = n // 2
    own_k = pltpu.make_async_copy(k_ref, kv_ref.at[0, me], local_sem.at[0])
    own_v = pltpu.make_async_copy(v_ref, kv_ref.at[1, me], local_sem.at[1])
    own_k.start()
    own_v.start()
    greet(n)
    own_k.wait()
    own_v.wait()

    def run_of(t):
        return lax.rem(me - way * t + n, n)

    def pieces(t):
        if t == half - 1:
            return [(core, u, u) for u in range(sub)]
        return [(a, u, a * sub + u) for u in range(sub) for a in range(2)]

    def hop(t, a, u, j):
        ref = kv_ref.at[a, run_of(t), pl.ds(u * part, part)]
        return send(ref, ref, ss.at[t, j], rs.at[t, j], ahead)

    def share(t):
        if t == half:
            ref = kv_ref.at[core, run_of(t)]
        else:
            ref = kv_ref.at[:, run_of(t)]
        return send(ref, ref, ps.at[t], pr.at[t], partner)

    def landed(t):
        run = lax.rem(me + way * t + n, n)
        if t == half:
            ref = kv_ref.at[1 - core, run]
        else:
            ref = kv_ref.at[:, run]
        return send(ref, ref, ps.at[t], pr.at[t], partner)

    for p in pieces(0):
        hop(0, *p).start()
    for t in range(half):
        later = pieces(t + 1) if t + 1 < half else []
        for a, u, j in pieces(t):
            ref = kv_ref.at[a, run_of(t + 1), pl.ds(u * part, part)]
            send(ref, ref, ss.at[t, j], rs.at[t, j], ahead).wait_recv()
            if t + 1 < half - 1:
                hop(t + 1, a, u, j).start()
        if t + 1 == half - 1:
            for p in later:
                hop(t + 1, *p).start()
        share(t + 1).start()
    for t in range(1, half + 1):
        landed(t).wait_recv()
        share(t).wait_send()
    for t in range(half):
        for p in pieces(t):
            hop(t, *p).wait_send()


def attend_kernel(scaling, picks, usable, q_ref, do_ref, kv_ref, dq_ref, tiles_ref, acc):
    i = pl.program_id(0)
    at = lax.axis_index("seq") * pl.num_programs(0) + i
    rows = q_ref.shape[0]
    per_pos = rows // BLK

    @pl.when(i == 0)
    def _():
        acc[...] = jnp.zeros_like(acc)

    q = q_ref[...]
    do = do_ref[...]
    names = [jnp.where(usable[t, at] > 0, picks[t, at], at) for t in range(TOPK)]
    ks = jnp.concatenate([kv_ref[0, b] for b in names], axis=0)
    vs = jnp.concatenate([kv_ref[1, b] for b in names], axis=0)
    nt = (((1,), (1,)), ((), ()))
    st = lax.dot_general(ks, q, nt, preferred_element_type=jnp.float32)
    key_at = lax.broadcasted_iota(jnp.int32, (BLK, rows), 0)
    query_at = lax.broadcasted_iota(jnp.int32, (BLK, rows), 1) // per_pos
    low = jnp.float32(-1e30)
    parts = [jnp.where(key_at <= query_at, st[:BLK], low)]
    for t in range(1, TOPK):
        bias = jnp.where(usable[t, at] > 0, jnp.float32(0.0), low)
        parts.append(st[t * BLK : (t + 1) * BLK] + bias)
    st = jnp.concatenate(parts, axis=0)
    top = jnp.max(st, axis=0, keepdims=True)
    w = jnp.exp2((st - top) * jnp.float32(scaling * LOG2E))
    inv = 1.0 / jnp.sum(w, axis=0, keepdims=True)
    p = w * inv
    dp = lax.dot_general(vs, do, nt, preferred_element_type=jnp.float32)
    delta = jnp.sum(p * dp, axis=0, keepdims=True)
    dsc = (p * (dp - delta)).astype(jnp.bfloat16)
    pb = p.astype(jnp.bfloat16)
    dqt = lax.dot_general(ks, dsc, (((0,), (0,)), ((), ())), preferred_element_type=jnp.float32)
    dq_ref[...] = (dqt.T * scaling).astype(jnp.bfloat16)
    dk = jnp.dot(dsc, q, preferred_element_type=jnp.float32) * scaling
    dv = jnp.dot(pb, do, preferred_element_type=jnp.float32)
    for t in range(TOPK):
        acc[0, names[t]] += dk[t * BLK : (t + 1) * BLK]
        acc[1, names[t]] += dv[t * BLK : (t + 1) * BLK]

    @pl.when(i == pl.num_programs(0) - 1)
    def _():
        tiles_ref[...] = acc[...].astype(jnp.bfloat16)


def reduce_kernel(n, sub, tiles, out, peer, put, got, mine, theirs, ss, rs, ps, pr, fs, fr):
    me = lax.axis_index("seq")
    core = lax.axis_index("inner")
    way = 1 - 2 * core
    ahead = {"seq": lax.rem(me - way + n, n)}
    partner = {"inner": 1 - core}
    part = tiles.shape[2] // sub
    half = n // 2
    f32, bf16 = jnp.float32, jnp.bfloat16
    greet(n)

    def owner(t, way):
        return lax.rem(me - way * (half - t) + 2 * n, n)

    def hand(t):
        run = owner(t, -way)
        if t == 0:
            src, dst = tiles.at[1 - core, run], peer.at[1 - core, t]
        else:
            src, dst = tiles.at[:, run], peer.at[:, t]
        return send(src, dst, ps.at[t], pr.at[t], partner)

    def landed(t):
        if t == 0:
            ref = peer.at[core, t]
        else:
            ref = peer.at[:, t]
        return send(ref, ref, ps.at[t], pr.at[t], partner)

    def pieces(t):
        if t == 0:
            return [(core, u, u) for u in range(sub)]
        return [(a, u, a * sub + u) for u in range(sub) for a in range(2)]

    def hop(t, a, u, j):
        s = pl.ds(u * part, part)
        return send(put.at[a, t, s], got.at[a, t, s], ss.at[t, j], rs.at[t, j], ahead)

    for t in range(half):
        hand(t).start()
    for t in range(half):
        landed(t).wait_recv()
        run = owner(t, way)
        if t == 1:
            for p in pieces(0):
                hop(0, *p).wait_recv()
        for a, u, j in pieces(t):
            s = pl.ds(u * part, part)
            val = tiles[a, run, s, :].astype(f32) + peer[a, t, s, :].astype(f32)
            if t == 1:
                come = got[a, 0, s, :].astype(f32)
                val = val + jnp.where(core == a, come, 0.0)
            elif t > 1:
                hop(t - 1, a, u, j).wait_recv()
                val = val + got[a, t - 1, s, :].astype(f32)
            put[a, t, s, :] = val.astype(bf16)
            hop(t, a, u, j).start()
    swaps = []
    for a, u, j in pieces(half - 1):
        s = pl.ds(u * part, part)
        hop(half - 1, a, u, j).wait_recv()
        mine[a, s, :] = (tiles[a, me, s, :].astype(f32) + got[a, half - 1, s, :].astype(f32)).astype(bf16)
        c = send(mine.at[a, s], theirs.at[a, s], fs.at[j], fr.at[j], partner)
        c.start()
        swaps.append((c, a, s))
    for c, a, s in swaps:
        c.wait_recv()
        out[a, s, :] = (mine[a, s, :].astype(f32) + theirs[a, s, :].astype(f32)).astype(bf16)
    for c, a, s in swaps:
        c.wait_send()
    for t in range(half):
        hand(t).wait_send()
        for p in pieces(t):
            hop(t, *p).wait_send()


def vmem():
    return pl.BlockSpec(memory_space=pltpu.VMEM)


def anywhere():
    return pl.BlockSpec(memory_space=pl.ANY)


def per_device(queries, grad_out, keys, values, indices, valid):
    tokens, _, heads_here, width = queries.shape
    n = lax.axis_size("seq")
    blocks = tokens // BLK
    total_blocks = n * blocks
    scaling = 1.0 / math.sqrt(width)
    rows = BLK * heads_here
    half = n // 2
    dma = pltpu.SemaphoreType.DMA
    bf16, f32 = jnp.bfloat16, jnp.float32
    picks, usable = indices[0].T, valid[0].T

    kv = pl.pallas_call(
        functools.partial(gather_kernel, n, SUB),
        out_shape=jax.ShapeDtypeStruct((2, n, tokens, width), bf16),
        in_specs=[anywhere()] * 2,
        out_specs=vmem(),
        scratch_shapes=[
            dma((2,)),
            dma((half, 2 * SUB)), dma((half, 2 * SUB)),
            dma((half + 1,)), dma((half + 1,)),
        ],
        compiler_params=pltpu.CompilerParams(collective_id=1, has_side_effects=True),
    )(keys[:, 0], values[:, 0])

    q2 = queries.reshape(tokens * heads_here, width)
    do2 = grad_out.reshape(tokens * heads_here, width)
    full = (2, total_blocks, BLK, width)
    whole = lambda i, *_: (0, 0, 0, 0)
    by_block = pl.BlockSpec((rows, width), lambda i, *_: (i, 0))
    dq, tiles = pl.pallas_call(
        functools.partial(attend_kernel, scaling),
        out_shape=(
            jax.ShapeDtypeStruct((tokens * heads_here, width), bf16),
            jax.ShapeDtypeStruct(full, bf16),
        ),
        grid_spec=pltpu.PrefetchScalarGridSpec(
            num_scalar_prefetch=2,
            grid=(blocks,),
            in_specs=[by_block, by_block, pl.BlockSpec(full, whole)],
            out_specs=[by_block, pl.BlockSpec(full, whole)],
            scratch_shapes=[pltpu.VMEM(full, f32)],
        ),
        compiler_params=pltpu.CompilerParams(
            dimension_semantics=("arbitrary",), vmem_limit_bytes=60 * 2**20
        ),
    )(picks, usable, q2, do2, kv.reshape(full))

    own = pl.pallas_call(
        functools.partial(reduce_kernel, n, SUB),
        out_shape=jax.ShapeDtypeStruct((2, tokens, width), bf16),
        in_specs=[vmem()],
        out_specs=vmem(),
        scratch_shapes=[
            pltpu.VMEM((2, half, tokens, width), bf16),
            pltpu.VMEM((2, half, tokens, width), bf16),
            pltpu.VMEM((2, half, tokens, width), bf16),
            pltpu.VMEM((2, tokens, width), bf16),
            pltpu.VMEM((2, tokens, width), bf16),
            dma((half, 2 * SUB)), dma((half, 2 * SUB)),
            dma((half,)), dma((half,)),
            dma((2 * SUB,)), dma((2 * SUB,)),
        ],
        compiler_params=pltpu.CompilerParams(
            collective_id=2, has_side_effects=True, vmem_limit_bytes=60 * 2**20
        ),
    )(tiles.reshape(2, n, tokens, width))
    gk, gv = own[0], own[1]
    return (
        dq.reshape(tokens, 1, heads_here, width),
        gk.reshape(tokens, 1, width),
        gv.reshape(tokens, 1, width),
    )


def solution(mesh):
    return jax.shard_map(
        per_device,
        mesh=mesh,
        in_specs=(
            P(("groups", "seq"), "head", "inner", None),
            P(("groups", "seq"), "head", "inner", None),
            P(("groups", "seq"), "head", None),
            P(("groups", "seq"), "head", None),
            P("head", "groups", None),
            P("head", "groups", None),
        ),
        out_specs=(
            P(("groups", "seq"), "head", "inner", None),
            P(("groups", "seq"), "head", None),
            P(("groups", "seq"), "head", None),
        ),
        check_vma=False,
    )
```

time: 143 us -> 133 us (0.930)
  Pallas kernels: 140 us -> 130 us
    pallas_call x2, Pallas kernels: 123 us -> 112 us  [the longest x1 74.6 us: per_device(): pl.pallas_call(functools.partial(gather_kernel, n, SUB), out_shape=jax.Sh...]
where the time goes in v5:
time: 133 us; the launch traced here: 132 us
  Pallas kernels  130 us (98%)
  local copies, waits for them, and re-layouts  1.69 us (1%)
    pallas_call x1, Pallas kernels, per_device(): pl.pallas_call(functools.partial(gather_kernel, n, SUB), out_shape=jax.Sh...  74.6 us
    pallas_call x1, Pallas kernels, per_device(): pl.pallas_call(functools.partial(reduce_kernel, n, SUB), out_shape=jax.Sh...  37.8 us
    pallas_call x1, Pallas kernels, per_device(): pl.pallas_call(functools.partial(attend_kernel, scaling), out_shape=(jax....  17.5 us

profile of v5, /device:TPU:65, one launch (start us, length us, event | category | flops | bytes accessed | tf_op | source)
XLA Modules:
  0.0 132.3 jit_solution(18174877112879433099)
XLA Ops:
  0.6 74.6 %shard_map.85 = bf16[2,16,512,128]{3,2,1,0:T(8,128)(2,1)} custom-call(bf16[512,128]{1,0:T(8,128)(2,1)} %bitcast.23, bf16[512,128]{1,0:T(8,128)(2,1)} %bitcast.24), custom_call_target="tpu_custom_call" | custom-call | tf_op jit(solution)/shard_map/pallas_call | solution.py:240
  75.3 17.5 %shard_map.86 = (bf16[2048,128]{1,0:T(8,128)(2,1)}, bf16[2,128,64,128]{3,2,1,0:T(8,128)(2,1)}) custom-call(s32[16,128]{1,0:T(8,128)} %bitcast.25, s32[16,128]{1,0:T(8,128)} %bitcast.26, bf16[2048,128]{1,0:T(8,128)(2,1)} %bitcast.21, bf16[2048,128]{1,0:T(8,128)(2,1)} %bitcast.22, bf16[2,128,64,128]{3,2,1,0:T(8,128)(2,1)} %bitcast.19), custom_call_target="tpu_custom_call" | custom-call | tf_op jit(solution)/shard_map/pallas_call | solution.py:258
  92.8 37.8 %shard_map.87 = bf16[2,512,128]{2,1,0:T(8,128)(2,1)} custom-call(bf16[2,16,512,128]{3,2,1,0:T(8,128)(2,1)} %bitcast.20), custom_call_target="tpu_custom_call" | custom-call | tf_op jit(solution)/shard_map/pallas_call | solution.py:276
  130.7 1.7 %slice_bitcast_fusion = (bf16[512,1,128]{2,0,1:T(8,128)(2,1)}, bf16[512,1,128]{2,0,1:T(8,128)(2,1)}) fusion(bf16[2,512,128]{2,1,0:T(8,128)(2,1)} %shard_map.87), kind=kLoop, calls=%fused_computation | loop fusion | bytes 524288 | tf_op jit(solution)/shard_map/reshape;squeeze | solution.py:299

commit v6 on v5

--- a/solution.py
+++ b/solution.py
@@ -247,7 +247,7 @@
             dma((half, 2 * SUB)), dma((half, 2 * SUB)),
             dma((half + 1,)), dma((half + 1,)),
         ],
-        compiler_params=pltpu.CompilerParams(collective_id=1, has_side_effects=True),
+        compiler_params=pltpu.CompilerParams(collective_id=1, has_side_effects=True, vmem_limit_bytes=12 * 2**20),
     )(keys[:, 0], values[:, 0])
 
     q2 = queries.reshape(tokens * heads_here, width)
@@ -269,7 +269,7 @@
             scratch_shapes=[pltpu.VMEM(full, f32)],
         ),
         compiler_params=pltpu.CompilerParams(
-            dimension_semantics=("arbitrary",), vmem_limit_bytes=60 * 2**20
+            dimension_semantics=("arbitrary",), vmem_limit_bytes=34 * 2**20
         ),
     )(picks, usable, q2, do2, kv.reshape(full))
 
@@ -289,7 +289,7 @@
             dma((2 * SUB,)), dma((2 * SUB,)),
         ],
         compiler_params=pltpu.CompilerParams(
-            collective_id=2, has_side_effects=True, vmem_limit_bytes=60 * 2**20
+            collective_id=2, has_side_effects=True, vmem_limit_bytes=28 * 2**20
         ),
     )(tiles.reshape(2, n, tokens, width))
     gk, gv = own[0], own[1]

time: 133 us -> 125 us (0.940)
  Pallas kernels: 130 us -> 122 us
    pallas_call x1, Pallas kernels: 17.5 us -> 13.7 us  [per_device(): pl.pallas_call(functools.partial(attend_kernel, scaling), out_shape=(jax....]
    pallas_call x1, Pallas kernels: 37.8 us -> 35 us  [per_device(): pl.pallas_call(functools.partial(reduce_kernel, n, SUB), out_shape=jax.Sh...]
    unnamed x0 -> x12, local copies, waits for them, and re-layouts: none -> 1.9 us
    pallas_call x1, Pallas kernels: 74.6 us -> 73.1 us  [per_device(): pl.pallas_call(functools.partial(gather_kernel, n, SUB), out_shape=jax.Sh...]
where the time goes in v6:
time: 125 us
  Pallas kernels  122 us (98%)
  local copies, waits for them, and re-layouts  2.62 us (2%)
    pallas_call x1, Pallas kernels, per_device(): pl.pallas_call(functools.partial(gather_kernel, n, SUB), out_shape=jax.Sh...  73.1 us
    pallas_call x1, Pallas kernels, per_device(): pl.pallas_call(functools.partial(reduce_kernel, n, SUB), out_shape=jax.Sh...  35 us
    pallas_call x1, Pallas kernels, per_device(): pl.pallas_call(functools.partial(attend_kernel, scaling), out_shape=(jax....  13.7 us

profile of v6, /device:TPU:65, one launch (start us, length us, event | category | flops | bytes accessed | tf_op | source)
XLA Modules:
  0.0 125.2 jit_solution(17122350266094555961)
XLA Ops:
  0.6 0.0 copy-start.1
  0.6 0.0 copy-start
  0.7 0.0 copy-start.2
  0.7 1.0 copy-done.2
  1.6 0.0 copy-start.3
  1.6 0.9 copy-done.3
  2.5 0.0 copy-start.4
  2.5 0.0 copy-start.5
  2.6 73.1 %shard_map.85 = bf16[2,16,512,128]{3,2,1,0:T(8,128)(2,1)S(1)} custom-call(bf16[512,128]{1,0:T(8,128)(2,1)S(1)} %bitcast.23, bf16[512,128]{1,0:T(8,128)(2,1)S(1)} %bitcast.24), custom_call_target="tpu_custom_call" | custom-call | tf_op jit(solution)/shard_map/pallas_call | solution.py:240
  75.7 0.0 copy-done.1
  75.7 0.0 copy-done
  75.7 0.0 copy-done.4
  75.7 0.0 copy-done.5
  75.7 13.7 %shard_map.86 = (bf16[2048,128]{1,0:T(8,128)(2,1)}, bf16[2,128,64,128]{3,2,1,0:T(8,128)(2,1)S(1)}) custom-call(s32[16,128]{1,0:T(8,128)S(1)} %bitcast.25, s32[16,128]{1,0:T(8,128)S(1)} %bitcast.26, bf16[2048,128]{1,0:T(8,128)(2,1)S(1)} %bitcast.21, bf16[2048,128]{1,0:T(8,128)(2,1)S(1)} %bitcast.22, bf16[2,128,64,128]{3,2,1,0:T(8,128)(2,1)S(1)} %bitcast.19), custom_call_target="tpu_custom_call" | custom-call | tf_op jit(solution)/shard_map/pallas_call | solution.py:258
  89.4 35.0 %shard_map.87 = bf16[2,512,128]{2,1,0:T(8,128)(2,1)S(1)} custom-call(bf16[2,16,512,128]{3,2,1,0:T(8,128)(2,1)S(1)} %bitcast.20), custom_call_target="tpu_custom_call" | custom-call | tf_op jit(solution)/shard_map/pallas_call | solution.py:276
  124.5 0.7 slice_bitcast_fusion
Async XLA Ops:
  0.6 75.1 %copy-start.1 = (bf16[512,1,4,128]{3,2,1,0:T(4,128)(2,1)S(1)}, bf16[512,1,4,128]{3,2,1,0:T(4,128)(2,1)}, u32[]{:S(2)}) copy-start(bf16[512,1,4,128]{3,2,1,0:T(4,128)(2,1)} %param.7) | copy-start | bytes 1572868
  0.6 75.1 %copy-start = (bf16[512,1,4,128]{3,2,1,0:T(4,128)(2,1)S(1)}, bf16[512,1,4,128]{3,2,1,0:T(4,128)(2,1)}, u32[]{:S(2)}) copy-start(bf16[512,1,4,128]{3,2,1,0:T(4,128)(2,1)} %param.6) | copy-start | bytes 1572868
  0.7 1.0 copy-start.2
  1.6 0.9 copy-start.3
  2.5 73.2 %copy-start.4 = (s32[1,128,16]{1,2,0:T(8,128)S(1)}, s32[1,128,16]{1,2,0:T(8,128)}, u32[]{:S(2)}) copy-start(s32[1,128,16]{1,2,0:T(8,128)} %param.10) | copy-start | bytes 24580
  2.5 73.2 %copy-start.5 = (s32[1,128,16]{1,2,0:T(8,128)S(1)}, s32[1,128,16]{1,2,0:T(8,128)}, u32[]{:S(2)}) copy-start(s32[1,128,16]{1,2,0:T(8,128)} %param.11) | copy-start | bytes 24580

commit v7 on v6

--- a/solution.py
+++ b/solution.py
@@ -11,6 +11,7 @@
 BLK = 64
 TOPK = 16
 SUB = 4
+TOGETHER = 2
 MESH = pl.DeviceIdType.MESH
 LOG2E = 1.4426950408889634
 
@@ -95,23 +96,15 @@
             hop(t, *p).wait_send()
 
 
-def attend_kernel(scaling, picks, usable, q_ref, do_ref, kv_ref, dq_ref, tiles_ref, acc):
-    i = pl.program_id(0)
-    at = lax.axis_index("seq") * pl.num_programs(0) + i
-    rows = q_ref.shape[0]
+def attend_block(scaling, at, picks, usable, q, do, kv_ref):
+    rows = q.shape[0]
     per_pos = rows // BLK
-
-    @pl.when(i == 0)
-    def _():
-        acc[...] = jnp.zeros_like(acc)
-
-    q = q_ref[...]
-    do = do_ref[...]
     names = [jnp.where(usable[t, at] > 0, picks[t, at], at) for t in range(TOPK)]
     ks = jnp.concatenate([kv_ref[0, b] for b in names], axis=0)
     vs = jnp.concatenate([kv_ref[1, b] for b in names], axis=0)
     nt = (((1,), (1,)), ((), ()))
     st = lax.dot_general(ks, q, nt, preferred_element_type=jnp.float32)
+    dp = lax.dot_general(vs, do, nt, preferred_element_type=jnp.float32)
     key_at = lax.broadcasted_iota(jnp.int32, (BLK, rows), 0)
     query_at = lax.broadcasted_iota(jnp.int32, (BLK, rows), 1) // per_pos
     low = jnp.float32(-1e30)
@@ -124,19 +117,38 @@
     w = jnp.exp2((st - top) * jnp.float32(scaling * LOG2E))
     inv = 1.0 / jnp.sum(w, axis=0, keepdims=True)
     p = w * inv
-    dp = lax.dot_general(vs, do, nt, preferred_element_type=jnp.float32)
     delta = jnp.sum(p * dp, axis=0, keepdims=True)
     dsc = (p * (dp - delta)).astype(jnp.bfloat16)
     pb = p.astype(jnp.bfloat16)
     dqt = lax.dot_general(ks, dsc, (((0,), (0,)), ((), ())), preferred_element_type=jnp.float32)
-    dq_ref[...] = (dqt.T * scaling).astype(jnp.bfloat16)
+    dq = (dqt.T * scaling).astype(jnp.bfloat16)
     dk = jnp.dot(dsc, q, preferred_element_type=jnp.float32) * scaling
     dv = jnp.dot(pb, do, preferred_element_type=jnp.float32)
-    for t in range(TOPK):
-        acc[0, names[t]] += dk[t * BLK : (t + 1) * BLK]
-        acc[1, names[t]] += dv[t * BLK : (t + 1) * BLK]
-
-    @pl.when(i == pl.num_programs(0) - 1)
+    return names, dq, dk, dv
+
+
+def attend_kernel(scaling, rows, picks, usable, q_ref, do_ref, kv_ref, dq_ref, tiles_ref, acc):
+    i = pl.program_id(0)
+    steps = pl.num_programs(0)
+    here = q_ref.shape[0] // rows
+    at = (lax.axis_index("seq") * steps + i) * here
+
+    @pl.when(i == 0)
+    def _():
+        acc[...] = jnp.zeros_like(acc)
+
+    done = []
+    for b in range(here):
+        s = slice(b * rows, (b + 1) * rows)
+        done.append(attend_block(scaling, at + b, picks, usable, q_ref[s], do_ref[s], kv_ref))
+    for b in range(here):
+        names, dq, dk, dv = done[b]
+        dq_ref[b * rows : (b + 1) * rows] = dq
+        for t in range(TOPK):
+            acc[0, names[t]] += dk[t * BLK : (t + 1) * BLK]
+            acc[1, names[t]] += dv[t * BLK : (t + 1) * BLK]
+
+    @pl.when(i == steps - 1)
     def _():
         tiles_ref[...] = acc[...].astype(jnp.bfloat16)
 
@@ -240,7 +252,7 @@
     kv = pl.pallas_call(
         functools.partial(gather_kernel, n, SUB),
         out_shape=jax.ShapeDtypeStruct((2, n, tokens, width), bf16),
-        in_specs=[anywhere()] * 2,
+        in_specs=[pl.BlockSpec(memory_space=pltpu.HBM)] * 2,
         out_specs=vmem(),
         scratch_shapes=[
             dma((2,)),
@@ -254,16 +266,16 @@
     do2 = grad_out.reshape(tokens * heads_here, width)
     full = (2, total_blocks, BLK, width)
     whole = lambda i, *_: (0, 0, 0, 0)
-    by_block = pl.BlockSpec((rows, width), lambda i, *_: (i, 0))
+    by_block = pl.BlockSpec((TOGETHER * rows, width), lambda i, *_: (i, 0))
     dq, tiles = pl.pallas_call(
-        functools.partial(attend_kernel, scaling),
+        functools.partial(attend_kernel, scaling, rows),
         out_shape=(
             jax.ShapeDtypeStruct((tokens * heads_here, width), bf16),
             jax.ShapeDtypeStruct(full, bf16),
         ),
         grid_spec=pltpu.PrefetchScalarGridSpec(
             num_scalar_prefetch=2,
-            grid=(blocks,),
+            grid=(blocks // TOGETHER,),
             in_specs=[by_block, by_block, pl.BlockSpec(full, whole)],
             out_specs=[by_block, pl.BlockSpec(full, whole)],
             scratch_shapes=[pltpu.VMEM(full, f32)],

time: 125 us -> 125 us (level)
  no operation moved by 1% of the time
where the time goes in v7:
time: 125 us; the launch traced here: 124 us
  Pallas kernels  121 us (97%)
  local copies, waits for them, and re-layouts  2.62 us (2%)
    pallas_call x1, Pallas kernels, per_device(): pl.pallas_call(functools.partial(gather_kernel, n, SUB), out_shape=jax.Sh...  73.1 us
    pallas_call x1, Pallas kernels, per_device(): pl.pallas_call(functools.partial(reduce_kernel, n, SUB), out_shape=jax.Sh...  35 us
    pallas_call x1, Pallas kernels, per_device(): pl.pallas_call(functools.partial(attend_kernel, scaling, rows), out_shape...  12.8 us

profile of v7, /device:TPU:65, one launch (start us, length us, event | category | flops | bytes accessed | tf_op | source)
XLA Modules:
  0.0 124.3 jit_solution(2097869713401977998)
XLA Ops:
  0.6 0.0 copy-start.1
  0.6 0.0 copy-start
  0.7 0.0 copy-start.2
  0.7 1.0 copy-done.2
  1.6 0.0 copy-start.3
  1.6 0.9 copy-done.3
  2.5 0.0 copy-start.4
  2.5 0.0 copy-start.5
  2.6 73.1 %shard_map.85 = bf16[2,16,512,128]{3,2,1,0:T(8,128)(2,1)S(1)} custom-call(bf16[512,128]{1,0:T(8,128)(2,1)S(1)} %bitcast.23, bf16[512,128]{1,0:T(8,128)(2,1)S(1)} %bitcast.24), custom_call_target="tpu_custom_call" | custom-call | tf_op jit(solution)/shard_map/pallas_call | solution.py:252
  75.7 0.0 copy-done.1
  75.7 0.0 copy-done
  75.7 0.0 copy-done.4
  75.7 0.0 copy-done.5
  75.7 12.8 %shard_map.86 = (bf16[2048,128]{1,0:T(8,128)(2,1)}, bf16[2,128,64,128]{3,2,1,0:T(8,128)(2,1)S(1)}) custom-call(s32[16,128]{1,0:T(8,128)S(1)} %bitcast.25, s32[16,128]{1,0:T(8,128)S(1)} %bitcast.26, bf16[2048,128]{1,0:T(8,128)(2,1)S(1)} %bitcast.21, bf16[2048,128]{1,0:T(8,128)(2,1)S(1)} %bitcast.22, bf16[2,128,64,128]{3,2,1,0:T(8,128)(2,1)S(1)} %bitcast.19), custom_call_target="tpu_custom_call" | custom-call | tf_op jit(solution)/shard_map/pallas_call | solution.py:270
  88.6 35.0 %shard_map.87 = bf16[2,512,128]{2,1,0:T(8,128)(2,1)S(1)} custom-call(bf16[2,16,512,128]{3,2,1,0:T(8,128)(2,1)S(1)} %bitcast.20), custom_call_target="tpu_custom_call" | custom-call | tf_op jit(solution)/shard_map/pallas_call | solution.py:288
  123.6 0.7 slice_bitcast_fusion
Async XLA Ops:
  0.6 75.1 %copy-start.1 = (bf16[512,1,4,128]{3,2,1,0:T(4,128)(2,1)S(1)}, bf16[512,1,4,128]{3,2,1,0:T(4,128)(2,1)}, u32[]{:S(2)}) copy-start(bf16[512,1,4,128]{3,2,1,0:T(4,128)(2,1)} %param.7) | copy-start | bytes 1572868
  0.6 75.1 %copy-start = (bf16[512,1,4,128]{3,2,1,0:T(4,128)(2,1)S(1)}, bf16[512,1,4,128]{3,2,1,0:T(4,128)(2,1)}, u32[]{:S(2)}) copy-start(bf16[512,1,4,128]{3,2,1,0:T(4,128)(2,1)} %param.6) | copy-start | bytes 1572868
  0.7 1.0 copy-start.2
  1.6 0.9 copy-start.3
  2.5 73.2 %copy-start.4 = (s32[1,128,16]{1,2,0:T(8,128)S(1)}, s32[1,128,16]{1,2,0:T(8,128)}, u32[]{:S(2)}) copy-start(s32[1,128,16]{1,2,0:T(8,128)} %param.10) | copy-start | bytes 24580
  2.5 73.2 %copy-start.5 = (s32[1,128,16]{1,2,0:T(8,128)S(1)}, s32[1,128,16]{1,2,0:T(8,128)}, u32[]{:S(2)}) copy-start(s32[1,128,16]{1,2,0:T(8,128)} %param.11) | copy-start | bytes 24580

commit v8 on v7

--- a/solution.py
+++ b/solution.py
@@ -11,7 +11,7 @@
 BLK = 64
 TOPK = 16
 SUB = 4
-TOGETHER = 2
+TOGETHER = 4
 MESH = pl.DeviceIdType.MESH
 LOG2E = 1.4426950408889634
 
@@ -32,29 +32,27 @@
     )
 
 
-def gather_kernel(n, sub, k_ref, v_ref, kv_ref, local_sem, ss, rs, ps, pr):
+def gather_kernel(n, sub, own_ref, kv_ref, local_sem, ss, rs, ps, pr):
     me = lax.axis_index("seq")
     core = lax.axis_index("inner")
     way = 1 - 2 * core
     ahead = {"seq": lax.rem(me + way + n, n)}
     partner = {"inner": 1 - core}
-    part = k_ref.shape[0] // sub
+    part = own_ref.shape[1] // sub
     half = n // 2
-    own_k = pltpu.make_async_copy(k_ref, kv_ref.at[0, me], local_sem.at[0])
-    own_v = pltpu.make_async_copy(v_ref, kv_ref.at[1, me], local_sem.at[1])
-    own_k.start()
-    own_v.start()
+    own = pltpu.make_async_copy(own_ref, kv_ref.at[:, me], local_sem)
+    own.start()
     greet(n)
-    own_k.wait()
-    own_v.wait()
+    own.wait()
 
     def run_of(t):
         return lax.rem(me - way * t + n, n)
 
     def pieces(t):
+        first = [(core, u, u) for u in range(sub)]
         if t == half - 1:
-            return [(core, u, u) for u in range(sub)]
-        return [(a, u, a * sub + u) for u in range(sub) for a in range(2)]
+            return first
+        return first + [(1 - core, u, sub + u) for u in range(sub)]
 
     def hop(t, a, u, j):
         ref = kv_ref.at[a, run_of(t), pl.ds(u * part, part)]
@@ -78,15 +76,12 @@
     for p in pieces(0):
         hop(0, *p).start()
     for t in range(half):
-        later = pieces(t + 1) if t + 1 < half else []
+        later = [j for _, _, j in pieces(t + 1)] if t + 1 < half else []
         for a, u, j in pieces(t):
             ref = kv_ref.at[a, run_of(t + 1), pl.ds(u * part, part)]
             send(ref, ref, ss.at[t, j], rs.at[t, j], ahead).wait_recv()
-            if t + 1 < half - 1:
+            if j in later:
                 hop(t + 1, a, u, j).start()
-        if t + 1 == half - 1:
-            for p in later:
-                hop(t + 1, *p).start()
         share(t + 1).start()
     for t in range(1, half + 1):
         landed(t).wait_recv()
@@ -183,9 +178,10 @@
         return send(ref, ref, ps.at[t], pr.at[t], partner)
 
     def pieces(t):
+        last = [(core, u, u) for u in range(sub)]
         if t == 0:
-            return [(core, u, u) for u in range(sub)]
-        return [(a, u, a * sub + u) for u in range(sub) for a in range(2)]
+            return last
+        return [(1 - core, u, sub + u) for u in range(sub)] + last
 
     def hop(t, a, u, j):
         s = pl.ds(u * part, part)
@@ -196,16 +192,10 @@
     for t in range(half):
         landed(t).wait_recv()
         run = owner(t, way)
-        if t == 1:
-            for p in pieces(0):
-                hop(0, *p).wait_recv()
         for a, u, j in pieces(t):
             s = pl.ds(u * part, part)
             val = tiles[a, run, s, :].astype(f32) + peer[a, t, s, :].astype(f32)
-            if t == 1:
-                come = got[a, 0, s, :].astype(f32)
-                val = val + jnp.where(core == a, come, 0.0)
-            elif t > 1:
+            if t > 1 or (t == 1 and j < sub):
                 hop(t - 1, a, u, j).wait_recv()
                 val = val + got[a, t - 1, s, :].astype(f32)
             put[a, t, s, :] = val.astype(bf16)
@@ -215,10 +205,10 @@
         s = pl.ds(u * part, part)
         hop(half - 1, a, u, j).wait_recv()
         mine[a, s, :] = (tiles[a, me, s, :].astype(f32) + got[a, half - 1, s, :].astype(f32)).astype(bf16)
-        c = send(mine.at[a, s], theirs.at[a, s], fs.at[j], fr.at[j], partner)
+        c = send(mine.at[a, s], theirs.at[a, s], fs.at[a * sub + u], fr.at[a * sub + u], partner)
         c.start()
         swaps.append((c, a, s))
-    for c, a, s in swaps:
+    for c, a, s in swaps[sub:] + swaps[:sub]:
         c.wait_recv()
         out[a, s, :] = (mine[a, s, :].astype(f32) + theirs[a, s, :].astype(f32)).astype(bf16)
     for c, a, s in swaps:
@@ -252,15 +242,15 @@
     kv = pl.pallas_call(
         functools.partial(gather_kernel, n, SUB),
         out_shape=jax.ShapeDtypeStruct((2, n, tokens, width), bf16),
-        in_specs=[pl.BlockSpec(memory_space=pltpu.HBM)] * 2,
+        in_specs=[anywhere()],
         out_specs=vmem(),
         scratch_shapes=[
-            dma((2,)),
+            dma,
             dma((half, 2 * SUB)), dma((half, 2 * SUB)),
             dma((half + 1,)), dma((half + 1,)),
         ],
         compiler_params=pltpu.CompilerParams(collective_id=1, has_side_effects=True, vmem_limit_bytes=12 * 2**20),
-    )(keys[:, 0], values[:, 0])
+    )(jnp.stack([keys[:, 0], values[:, 0]]))
 
     q2 = queries.reshape(tokens * heads_here, width)
     do2 = grad_out.reshape(tokens * heads_here, width)

time: 125 us -> 118 us (0.944)
  Pallas kernels: 121 us -> 115 us
  local copies, waits for them, and re-layouts: 2.62 us -> 0.73 us
    pallas_call x1, Pallas kernels: 73.1 us -> 70.3 us  [per_device(): pl.pallas_call(functools.partial(gather_kernel, n, SUB), out_shape=jax.Sh...]
    pallas_call x1, Pallas kernels: 35 us -> 32.5 us  [per_device(): pl.pallas_call(functools.partial(reduce_kernel, n, SUB), out_shape=jax.Sh...]
    unnamed x12 -> x8, local copies, waits for them, and re-layouts: 1.9 us -> 0.02 us
where the time goes in v8:
time: 118 us; the launch traced here: 117 us
  Pallas kernels  115 us (97%)
    pallas_call x1, Pallas kernels, per_device(): pl.pallas_call(functools.partial(gather_kernel, n, SUB), out_shape=jax.Sh...  70.3 us
    pallas_call x1, Pallas kernels, per_device(): pl.pallas_call(functools.partial(reduce_kernel, n, SUB), out_shape=jax.Sh...  32.5 us
    pallas_call x1, Pallas kernels, per_device(): pl.pallas_call(functools.partial(attend_kernel, scaling, rows), out_shape...  12.2 us

profile of v8, /device:TPU:65, one launch (start us, length us, event | category | flops | bytes accessed | tf_op | source)
XLA Modules:
  0.0 117.5 jit_solution(2299169294837597625)
XLA Ops:
  0.6 0.0 copy-start.3
  0.6 0.0 copy-start.2
  0.7 0.0 copy-start.1
  0.7 0.0 copy-start
  0.7 1.1 pad_maximum_fusion.own_ref
  1.8 70.3 %shard_map.85 = bf16[2,16,512,128]{3,2,1,0:T(8,128)(2,1)S(1)} custom-call(bf16[2,512,128]{2,1,0:T(8,128)(2,1)S(1)} %pad_maximum_fusion.own_ref), custom_call_target="tpu_custom_call" | custom-call | tf_op jit(solution)/shard_map/pallas_call | solution.py:242
  72.1 0.0 copy-done.3
  72.1 0.0 copy-done.2
  72.1 0.0 copy-done.1
  72.1 0.0 copy-done
  72.1 12.2 %shard_map.86 = (bf16[2048,128]{1,0:T(8,128)(2,1)}, bf16[2,128,64,128]{3,2,1,0:T(8,128)(2,1)S(1)}) custom-call(s32[16,128]{1,0:T(8,128)S(1)} %bitcast.23, s32[16,128]{1,0:T(8,128)S(1)} %bitcast.24, bf16[2048,128]{1,0:T(8,128)(2,1)S(1)} %bitcast.21, bf16[2048,128]{1,0:T(8,128)(2,1)S(1)} %bitcast.22, bf16[2,128,64,128]{3,2,1,0:T(8,128)(2,1)S(1)} %bitcast.19), custom_call_target="tpu_custom_call" | custom-call | tf_op jit(solution)/shard_map/pallas_call | solution.py:260
  84.3 32.5 %shard_map.87 = bf16[2,512,128]{2,1,0:T(8,128)(2,1)S(1)} custom-call(bf16[2,16,512,128]{3,2,1,0:T(8,128)(2,1)S(1)} %bitcast.20), custom_call_target="tpu_custom_call" | custom-call | tf_op jit(solution)/shard_map/pallas_call | solution.py:278
  116.7 0.7 slice_bitcast_fusion
Async XLA Ops:
  0.6 71.4 %copy-start.3 = (s32[1,128,16]{1,2,0:T(8,128)S(1)}, s32[1,128,16]{1,2,0:T(8,128)}, u32[]{:S(2)}) copy-start(s32[1,128,16]{1,2,0:T(8,128)} %param.11) | copy-start | bytes 24580
  0.6 71.4 %copy-start.2 = (s32[1,128,16]{1,2,0:T(8,128)S(1)}, s32[1,128,16]{1,2,0:T(8,128)}, u32[]{:S(2)}) copy-start(s32[1,128,16]{1,2,0:T(8,128)} %param.10) | copy-start | bytes 24580
  0.7 71.4 %copy-start.1 = (bf16[512,1,4,128]{3,2,1,0:T(4,128)(2,1)S(1)}, bf16[512,1,4,128]{3,2,1,0:T(4,128)(2,1)}, u32[]{:S(2)}) copy-start(bf16[512,1,4,128]{3,2,1,0:T(4,128)(2,1)} %param.7) | copy-start | bytes 1572868
  0.7 71.4 %copy-start = (bf16[512,1,4,128]{3,2,1,0:T(4,128)(2,1)S(1)}, bf16[512,1,4,128]{3,2,1,0:T(4,128)(2,1)}, u32[]{:S(2)}) copy-start(bf16[512,1,4,128]{3,2,1,0:T(4,128)(2,1)} %param.6) | copy-start | bytes 1572868

commit v9 on v8

--- a/solution.py
+++ b/solution.py
@@ -10,7 +10,8 @@
 
 BLK = 64
 TOPK = 16
-SUB = 4
+SUB = 8
+COARSE = 2
 TOGETHER = 4
 MESH = pl.DeviceIdType.MESH
 LOG2E = 1.4426950408889634
@@ -32,13 +33,18 @@
     )
 
 
+def cut(a, rows, count, j):
+    size = rows // count
+    return [(a, pl.ds(u * size, size), j + u) for u in range(count)]
+
+
 def gather_kernel(n, sub, own_ref, kv_ref, local_sem, ss, rs, ps, pr):
     me = lax.axis_index("seq")
     core = lax.axis_index("inner")
     way = 1 - 2 * core
     ahead = {"seq": lax.rem(me + way + n, n)}
     partner = {"inner": 1 - core}
-    part = own_ref.shape[1] // sub
+    rows = own_ref.shape[1]
     half = n // 2
     own = pltpu.make_async_copy(own_ref, kv_ref.at[:, me], local_sem)
     own.start()
@@ -49,13 +55,13 @@
         return lax.rem(me - way * t + n, n)
 
     def pieces(t):
-        first = [(core, u, u) for u in range(sub)]
+        first = cut(core, rows, sub, 0)
         if t == half - 1:
             return first
-        return first + [(1 - core, u, sub + u) for u in range(sub)]
-
-    def hop(t, a, u, j):
-        ref = kv_ref.at[a, run_of(t), pl.ds(u * part, part)]
+        return first + cut(1 - core, rows, COARSE, sub)
+
+    def hop(t, a, s, j):
+        ref = kv_ref.at[a, run_of(t), s]
         return send(ref, ref, ss.at[t, j], rs.at[t, j], ahead)
 
     def share(t):
@@ -77,11 +83,11 @@
         hop(0, *p).start()
     for t in range(half):
         later = [j for _, _, j in pieces(t + 1)] if t + 1 < half else []
-        for a, u, j in pieces(t):
-            ref = kv_ref.at[a, run_of(t + 1), pl.ds(u * part, part)]
+        for a, s, j in pieces(t):
+            ref = kv_ref.at[a, run_of(t + 1), s]
             send(ref, ref, ss.at[t, j], rs.at[t, j], ahead).wait_recv()
             if j in later:
-                hop(t + 1, a, u, j).start()
+                hop(t + 1, a, s, j).start()
         share(t + 1).start()
     for t in range(1, half + 1):
         landed(t).wait_recv()
@@ -154,7 +160,7 @@
     way = 1 - 2 * core
     ahead = {"seq": lax.rem(me - way + n, n)}
     partner = {"inner": 1 - core}
-    part = tiles.shape[2] // sub
+    rows = tiles.shape[2]
     half = n // 2
     f32, bf16 = jnp.float32, jnp.bfloat16
     greet(n)
@@ -178,13 +184,12 @@
         return send(ref, ref, ps.at[t], pr.at[t], partner)
 
     def pieces(t):
-        last = [(core, u, u) for u in range(sub)]
+        last = cut(core, rows, sub, 0)
         if t == 0:
             return last
-        return [(1 - core, u, sub + u) for u in range(sub)] + last
-
-    def hop(t, a, u, j):
-        s = pl.ds(u * part, part)
+        return cut(1 - core, rows, COARSE, sub) + last
+
+    def hop(t, a, s, j):
         return send(put.at[a, t, s], got.at[a, t, s], ss.at[t, j], rs.at[t, j], ahead)
 
     for t in range(half):
@@ -192,27 +197,27 @@
     for t in range(half):
         landed(t).wait_recv()
         run = owner(t, way)
-        for a, u, j in pieces(t):
-            s = pl.ds(u * part, part)
+        for a, s, j in pieces(t):
             val = tiles[a, run, s, :].astype(f32) + peer[a, t, s, :].astype(f32)
             if t > 1 or (t == 1 and j < sub):
-                hop(t - 1, a, u, j).wait_recv()
+                hop(t - 1, a, s, j).wait_recv()
                 val = val + got[a, t - 1, s, :].astype(f32)
             put[a, t, s, :] = val.astype(bf16)
-            hop(t, a, u, j).start()
-    swaps = []
-    for a, u, j in pieces(half - 1):
-        s = pl.ds(u * part, part)
-        hop(half - 1, a, u, j).wait_recv()
+            hop(t, a, s, j).start()
+    def swap(a):
+        return send(mine.at[a], theirs.at[a], fs.at[a], fr.at[a], partner)
+
+    for a, s, j in pieces(half - 1):
+        hop(half - 1, a, s, j).wait_recv()
         mine[a, s, :] = (tiles[a, me, s, :].astype(f32) + got[a, half - 1, s, :].astype(f32)).astype(bf16)
-        c = send(mine.at[a, s], theirs.at[a, s], fs.at[a * sub + u], fr.at[a * sub + u], partner)
-        c.start()
-        swaps.append((c, a, s))
-    for c, a, s in swaps[sub:] + swaps[:sub]:
-        c.wait_recv()
-        out[a, s, :] = (mine[a, s, :].astype(f32) + theirs[a, s, :].astype(f32)).astype(bf16)
-    for c, a, s in swaps:
-        c.wait_send()
+        if j == sub + COARSE - 1:
+            swap(1 - core).start()
+    swap(core).start()
+    for a in (core, 1 - core):
+        swap(a).wait_recv()
+        out[a] = (mine[a].astype(f32) + theirs[a].astype(f32)).astype(bf16)
+    for a in range(2):
+        swap(a).wait_send()
     for t in range(half):
         hand(t).wait_send()
         for p in pieces(t):
@@ -288,7 +293,7 @@
             pltpu.VMEM((2, tokens, width), bf16),
             dma((half, 2 * SUB)), dma((half, 2 * SUB)),
             dma((half,)), dma((half,)),
-            dma((2 * SUB,)), dma((2 * SUB,)),
+            dma((2,)), dma((2,)),
         ],
         compiler_params=pltpu.CompilerParams(
             collective_id=2, has_side_effects=True, vmem_limit_bytes=28 * 2**20

time: 118 us -> 123 us (1.042)
  Pallas kernels: 115 us -> 120 us
    pallas_call x1, Pallas kernels: 32.5 us -> 36.3 us  [per_device(): pl.pallas_call(functools.partial(reduce_kernel, n, SUB), out_shape=jax.Sh...]
    pallas_call x1, Pallas kernels: 70.3 us -> 71.8 us  [per_device(): pl.pallas_call(functools.partial(gather_kernel, n, SUB), out_shape=jax.Sh...]
where the time goes in v9:
time: 123 us
  Pallas kernels  120 us (98%)
    pallas_call x1, Pallas kernels, per_device(): pl.pallas_call(functools.partial(gather_kernel, n, SUB), out_shape=jax.Sh...  71.8 us
    pallas_call x1, Pallas kernels, per_device(): pl.pallas_call(functools.partial(reduce_kernel, n, SUB), out_shape=jax.Sh...  36.3 us
    pallas_call x1, Pallas kernels, per_device(): pl.pallas_call(functools.partial(attend_kernel, scaling, rows), out_shape...  12.2 us

profile of v9, /device:TPU:65, one launch (start us, length us, event | category | flops | bytes accessed | tf_op | source)
XLA Modules:
  0.0 122.7 jit_solution(17470042978814022101)
XLA Ops:
  0.6 0.0 copy-start.3
  0.6 0.0 copy-start.2
  0.7 0.0 copy-start.1
  0.7 0.0 copy-start
  0.7 1.1 pad_maximum_fusion.own_ref
  1.8 71.8 %shard_map.85 = bf16[2,16,512,128]{3,2,1,0:T(8,128)(2,1)S(1)} custom-call(bf16[2,512,128]{2,1,0:T(8,128)(2,1)S(1)} %pad_maximum_fusion.own_ref), custom_call_target="tpu_custom_call" | custom-call | tf_op jit(solution)/shard_map/pallas_call | solution.py:247
  73.5 0.0 copy-done.3
  73.5 0.0 copy-done.2
  73.5 0.0 copy-done.1
  73.6 0.0 copy-done
  73.6 12.2 %shard_map.86 = (bf16[2048,128]{1,0:T(8,128)(2,1)}, bf16[2,128,64,128]{3,2,1,0:T(8,128)(2,1)S(1)}) custom-call(s32[16,128]{1,0:T(8,128)S(1)} %bitcast.23, s32[16,128]{1,0:T(8,128)S(1)} %bitcast.24, bf16[2048,128]{1,0:T(8,128)(2,1)S(1)} %bitcast.21, bf16[2048,128]{1,0:T(8,128)(2,1)S(1)} %bitcast.22, bf16[2,128,64,128]{3,2,1,0:T(8,128)(2,1)S(1)} %bitcast.19), custom_call_target="tpu_custom_call" | custom-call | tf_op jit(solution)/shard_map/pallas_call | solution.py:265
  85.7 36.3 %shard_map.87 = bf16[2,512,128]{2,1,0:T(8,128)(2,1)S(1)} custom-call(bf16[2,16,512,128]{3,2,1,0:T(8,128)(2,1)S(1)} %bitcast.20), custom_call_target="tpu_custom_call" | custom-call | tf_op jit(solution)/shard_map/pallas_call | solution.py:283
  122.0 0.7 slice_bitcast_fusion
Async XLA Ops:
  0.6 72.9 %copy-start.3 = (s32[1,128,16]{1,2,0:T(8,128)S(1)}, s32[1,128,16]{1,2,0:T(8,128)}, u32[]{:S(2)}) copy-start(s32[1,128,16]{1,2,0:T(8,128)} %param.11) | copy-start | bytes 24580
  0.6 72.9 %copy-start.2 = (s32[1,128,16]{1,2,0:T(8,128)S(1)}, s32[1,128,16]{1,2,0:T(8,128)}, u32[]{:S(2)}) copy-start(s32[1,128,16]{1,2,0:T(8,128)} %param.10) | copy-start | bytes 24580
  0.7 72.9 %copy-start.1 = (bf16[512,1,4,128]{3,2,1,0:T(4,128)(2,1)S(1)}, bf16[512,1,4,128]{3,2,1,0:T(4,128)(2,1)}, u32[]{:S(2)}) copy-start(bf16[512,1,4,128]{3,2,1,0:T(4,128)(2,1)} %param.7) | copy-start | bytes 1572868
  0.7 72.9 %copy-start = (bf16[512,1,4,128]{3,2,1,0:T(4,128)(2,1)S(1)}, bf16[512,1,4,128]{3,2,1,0:T(4,128)(2,1)}, u32[]{:S(2)}) copy-start(bf16[512,1,4,128]{3,2,1,0:T(4,128)(2,1)} %param.6) | copy-start | bytes 1572868
